TPU v7x, 32 devices: a whole 2x2x4 slice. The times are simulated.
32 devices in a mesh: col: 8 (over z, y), row: 4 (over x, core).
Axes of the slice: x: 2, y: 2, z: 4, core: 2. Of those that a mesh axis runs over, the one named last changes fastest.
Arguments:
- x_in: bfloat16 [2, 192, 1536, 128], P(None, 'row', 'col')
- a_pre: bfloat16 [2, 192, 1536, 128], P(None, 'row', 'col')
- g_out: bfloat16 [2, 192, 1536, 128], P(None, 'row', 'col')
- w_one: bfloat16 [3, 3, 128, 128], replicated
- w_two: bfloat16 [3, 3, 128, 128], replicated
Outputs:
- output 1: bfloat16 [2, 192, 1536, 128], P(None, 'row', 'col')
- output 2: float32 [3, 3, 128, 128], replicated
- output 3: float32 [3, 3, 128, 128], replicated
All inputs are finite; a program needn't handle non-finite values.
Results may differ from a plain program's by a relative error of at most 0.001.
Values are sent between devices in bfloat16 or wider.
A program may use at most 1 GiB of HBM per device.

v0:
```python
import jax
import jax.numpy as jnp
from jax import lax
from jax.sharding import PartitionSpec as P

DATA_DIMS = ("NHWC", "HWOI", "NHWC")


def gelu_slope(pre_act):
    tanh_scale = 0.7978845608028654
    cube_coef = 0.044715
    tanh_val = jnp.tanh(tanh_scale * (pre_act + cube_coef * pre_act * pre_act * pre_act))
    return 0.5 * (1.0 + tanh_val) + 0.5 * pre_act * (1.0 - tanh_val * tanh_val) * tanh_scale * (1.0 + 3.0 * cube_coef * pre_act * pre_act)


def conv_valid(lhs_arr, rhs_arr):
    return lax.conv_general_dilated(lhs_arr, rhs_arr, (1, 1), "VALID", dimension_numbers=DATA_DIMS, preferred_element_type=jnp.float32)


def tap_grads(tile_in, grad_wide):
    row_count = tile_in.shape[1]
    col_count = tile_in.shape[2]
    return jnp.stack([jnp.stack([jnp.einsum("bhwi,bhwo->io", tile_in, grad_wide[:, 2 - tap_row:2 - tap_row + row_count, 2 - tap_col:2 - tap_col + col_count], preferred_element_type=jnp.float32) for tap_col in range(3)]) for tap_row in range(3)])


def shift_pairs(count):
    forward_pairs = [(source, source + 1) for source in range(count - 1)]
    backward_pairs = [(source + 1, source) for source in range(count - 1)]
    return forward_pairs, backward_pairs


def solution(mesh):
    row_down, row_up = shift_pairs(mesh.shape["row"])
    col_down, col_up = shift_pairs(mesh.shape["col"])

    def add_halo(tile):
        from_above = lax.ppermute(tile[:, -1:], "row", row_down)
        from_below = lax.ppermute(tile[:, :1], "row", row_up)
        tall = jnp.concatenate([from_above, tile, from_below], axis=1)
        from_left = lax.ppermute(tall[:, :, -1:], "col", col_down)
        from_right = lax.ppermute(tall[:, :, :1], "col", col_up)
        return jnp.concatenate([from_left, tall, from_right], axis=2)

    def local_step(x_tile, a_tile, g_tile, w_one, w_two):
        a_val = a_tile.astype(jnp.float32)
        z_act = jax.nn.gelu(a_val, approximate=True).astype(jnp.bfloat16)
        g_wide = add_halo(g_tile)
        d_z = conv_valid(g_wide, w_two[::-1, ::-1])
        w2_part = tap_grads(z_act, g_wide)
        d_a = (d_z * gelu_slope(a_val)).astype(jnp.bfloat16)
        grad_wide = add_halo(d_a)
        d_x = (conv_valid(grad_wide, w_one[::-1, ::-1]) + g_tile.astype(jnp.float32)).astype(jnp.bfloat16)
        w1_part = tap_grads(x_tile, grad_wide)
        d_w1, d_w2 = lax.psum((w1_part, w2_part), ("row", "col"))
        return d_x, d_w1, d_w2

    tile_spec = P(None, "row", "col", None)
    return jax.shard_map(local_step, mesh=mesh, in_specs=(tile_spec, tile_spec, tile_spec, P(), P()), out_specs=(tile_spec, P(), P()), check_vma=False)
```

profile of v0, /device:TPU:0, one launch (start us, length us, event | category | flops | bytes accessed | tf_op | source)
XLA Modules:
  0.0 362.7 jit_solution(17317703205614472824)
XLA Ops:
  8.2 2.4 collective-permute-start
  10.7 1.6 collective-permute-start.1
  12.2 7.5 %convolution_bitcast_fusion = f32[1,128,128]{2,1,0:T(8,128)S(1)} fusion(bf16[2,48,192,128]{3,2,1,0:T(8,128)(2,1)} %param.7, bf16[2,48,192,128]{3,2,1,0:T(8,128)(2,1)} %param.6), kind=kOutput, calls=%fused_computation.111 | convolution fusion | flops 627572736 | bytes 9502720 | tf_op jit(solution)/shard_map/bhwi,bhwo->io/dot_general | solution.py:23
  20.6 1.6 collective-permute-start.3
  22.2 5.2 %collective-permute-start.2 = (bf16[2,50,1,128]{3,2,1,0:T(2,128)(2,1)S(1)}, bf16[2,50,1,128]{3,2,1,0:T(2,128)(2,1)S(1)}, u32[]{:S(2)}, u32[]{:S(2)}) collective-permute-start(bf16[2,50,1,128]{3,2,1,0:T(2,128)(2,1)S(1)} %get-tuple-element.15), channel_id=1, source_target_pairs={{0,4},{4,8},{8,12},{12,16},{16,20},{20,24},{24,28},{1,5},{5,9},{9,... | collective-permute-start | bytes 76808 | tf_op jit(solution)/shard_map/ppermute | solution.py:40
  27.4 4.0 %fusion.97 = f32[1,128,128]{2,1,0:T(8,128)S(1)} fusion(bf16[2,1,192,128]{3,2,1,0:T(8,128)(2,1)S(1)} %collective-permute-done.1, bf16[2,48,192,128]{3,2,1,0:T(8,128)(2,1)S(1)} %bitcast.186, bf16[2,48,192,128]{3,2,1,0:T(8,128)(2,1)S(1)} %bitcast.192), kind=kOutput, calls=%fused_computation.105 | convolution fusion | flops 629932032 | bytes 9601024 | tf_op jit(solution)/shard_map/bhwi,bhwo->io/dot_general | solution.py:23
  31.4 4.0 %fusion.99 = f32[1,128,128]{2,1,0:T(8,128)S(1)} fusion(bf16[2,48,192,128]{3,2,1,0:T(8,128)(2,1)S(1)} %bitcast.186, bf16[2,1,192,128]{3,2,1,0:T(8,128)(2,1)S(1)} %collective-permute-done, bf16[2,48,192,128]{3,2,1,0:T(8,128)(2,1)S(1)} %bitcast.192), kind=kOutput, calls=%fused_computation.107 | convolution fusion | flops 629932032 | bytes 9601024 | tf_op jit(solution)/shard_map/bhwi,bhwo->io/dot_general | solution.py:23
  35.4 5.5 %maximum_bitcast_fusion = bf16[50,2,194,128]{3,2,0,1:T(8,128)(2,1)} fusion(bf16[2,50,1,128]{3,2,1,0:T(2,128)(2,1)S(1)} %collective-permute-done.3, bf16[2,50,192,128]{3,2,1,0:T(8,128)(2,1)S(1)} %constant_dynamic-update-slice_fusion, bf16[2,50,1,128]{3,2,1,0:T(2,128)(2,1)S(1)} %collective-permute-done.2), kind=kLoop, calls=%fused_computation.45 | loop fusion | flops 14899200 | bytes 9932800 | tf_op jit(solution)/shard_map/concatenate | solution.py:42
  41.0 8.7 %copy.42 = bf16[50,2,194,128]{3,1,2,0:T(2,128)(2,1)} copy(bf16[50,2,194,128]{3,2,0,1:T(8,128)(2,1)} %maximum_bitcast_fusion) | data formatting | bytes 9932800
  49.7 8.6 %pad.clone = bf16[50,2,200,128]{3,1,2,0:T(2,128)(2,1)} pad(bf16[50,2,194,128]{3,1,2,0:T(2,128)(2,1)} %copy.42, bf16[]{:T(256)} %constant.10), padding=0_0x0_0x0_6x0_0 | pad | bytes 10086402 | tf_op jit(solution)/shard_map/concatenate | solution.py:42
  58.3 1.3 slice.118
  59.6 6.9 %fusion.19 = bf16[50,2,8,27,128]{4,1,3,2,0:T(2,128)(2,1)S(1)} fusion(bf16[50,2,7,2,128]{4,1,3,2,0:T(2,128)(2,1)S(1)} %slice.118, bf16[50,2,8,25,128]{4,1,3,2,0:T(2,128)(2,1)} %bitcast.184), kind=kLoop, calls=%fused_computation.37 | loop fusion | flops 16588800 | bytes 11008000 | tf_op jit(solution)/shard_map/conv_general_dilated | solution.py:17
  66.5 14.2 %broadcast_select_fusion.1 = f32[48,16,25,128]{3,1,2,0:T(8,128)} fusion(pred[16,25]{0,1:T(8,128)(4,1)S(1)} %copy-done.4, bf16[3,3,128,128]{3,2,1,0:T(8,128)(2,1)S(1)} %copy-done, bf16[50,2,8,27,128]{4,1,3,2,0:T(2,128)(2,1)S(1)} %fusion.19), kind=kOutput, calls=%fused_computation.50 | convolution fusion | flops 5664768000 | bytes 15655312 | tf_op jit(solution)/shard_map/conv_general_dilated | solution.py:17
  80.7 7.0 %copy.15 = f32[48,16,25,128]{3,0,2,1:T(8,128)S(1)} copy(f32[48,16,25,128]{3,1,2,0:T(8,128)} %broadcast_select_fusion.1) | data formatting | bytes 19660800 | tf_op jit(solution)/shard_map/conv_general_dilated | solution.py:17
  87.7 4.3 %slice.119 = f32[48,2,192,128]{3,0,2,1:T(8,128)} slice(f32[48,2,200,128]{3,0,2,1:T(8,128)S(1)} %bitcast.180), slice={[0:48], [0:2], [0:192], [0:128]} | slice | bytes 18874368 | tf_op jit(solution)/shard_map/conv_general_dilated | solution.py:17
  92.0 9.6 %fusion.9 = bf16[2,48,192,128]{3,2,1,0:T(8,128)(2,1)S(1)} fusion(bf16[2,48,192,128]{3,2,1,0:T(8,128)(2,1)S(1)} %bitcast.194, f32[48,2,192,128]{3,0,2,1:T(8,128)} %slice.119), kind=kLoop, calls=%fused_computation.21 | loop fusion | flops 47185920 | bytes 18874368 | tf_op jit(solution)/shard_map/convert_element_type | solution.py:50
  101.6 1.3 collective-permute-start.5
  102.9 5.3 %collective-permute-start.4 = (bf16[2,1,192,128]{3,2,1,0:T(8,128)(2,1)S(1)}, bf16[2,1,192,128]{3,2,1,0:T(8,128)(2,1)S(1)}, u32[]{:S(2)}, u32[]{:S(2)}) collective-permute-start(bf16[2,1,192,128]{3,2,1,0:T(8,128)(2,1)S(1)} %get-tuple-element.17), channel_id=1, source_target_pairs={{0,1},{1,2},{2,3},{4,5},{5,6},{6,7},{8,9},{9,10},{10,11},{12,13},{... | collective-permute-start | bytes 294920 | tf_op jit(solution)/shard_map/ppermute | solution.py:37
  108.2 1.5 convolution_bitcast_fusion.1
  109.8 5.1 %fusion.100 = f32[1,128,128]{2,1,0:T(8,128)S(1)} fusion(bf16[2,50,192,128]{3,2,1,0:T(8,128)(2,1)S(1)} %bitcast.190, bf16[2,50,1,128]{3,2,1,0:T(2,128)(2,1)S(1)} %collective-permute-done.2, bf16[2,48,192,128]{3,2,1,0:T(8,128)(2,1)S(1)} %bitcast.194), kind=kOutput, calls=%fused_computation.108 | convolution fusion | flops 637009920 | bytes 9724928 | tf_op jit(solution)/shard_map/bhwi,bhwo->io/dot_general | solution.py:23
  114.9 5.1 %fusion.98 = f32[1,128,128]{2,1,0:T(8,128)S(1)} fusion(bf16[2,50,1,128]{3,2,1,0:T(2,128)(2,1)S(1)} %collective-permute-done.3, bf16[2,50,192,128]{3,2,1,0:T(8,128)(2,1)S(1)} %bitcast.190, bf16[2,48,192,128]{3,2,1,0:T(8,128)(2,1)S(1)} %bitcast.194), kind=kOutput, calls=%fused_computation.106 | convolution fusion | flops 637009920 | bytes 9724928 | tf_op jit(solution)/shard_map/bhwi,bhwo->io/dot_general | solution.py:23
  120.0 5.3 %fusion.107 = f32[1,128,128]{2,1,0:T(8,128)S(1)} fusion(bf16[2,50,1,128]{3,2,1,0:T(2,128)(2,1)S(1)} %collective-permute-done.3, bf16[2,50,192,128]{3,2,1,0:T(8,128)(2,1)S(1)} %bitcast.190, bf16[2,48,192,128]{3,2,1,0:T(8,128)(2,1)S(1)} %bitcast.194), kind=kOutput, calls=%fused_computation.113 | convolution fusion | flops 637009920 | bytes 9724928 | tf_op jit(solution)/shard_map/bhwi,bhwo->io/dot_general | solution.py:23
  125.3 5.1 %fusion.110 = f32[1,128,128]{2,1,0:T(8,128)S(1)} fusion(bf16[2,50,1,128]{3,2,1,0:T(2,128)(2,1)S(1)} %collective-permute-done.3, bf16[2,50,192,128]{3,2,1,0:T(8,128)(2,1)S(1)} %bitcast.190, bf16[2,48,192,128]{3,2,1,0:T(8,128)(2,1)S(1)} %bitcast.194), kind=kOutput, calls=%fused_computation.114 | convolution fusion | flops 637009920 | bytes 9724928 | tf_op jit(solution)/shard_map/bhwi,bhwo->io/dot_general | solution.py:23
  130.4 5.5 %fusion.113 = f32[1,128,128]{2,1,0:T(8,128)S(1)} fusion(bf16[2,50,1,128]{3,2,1,0:T(2,128)(2,1)S(1)} %collective-permute-done.2, bf16[2,50,192,128]{3,2,1,0:T(8,128)(2,1)S(1)} %bitcast.190, bf16[2,48,192,128]{3,2,1,0:T(8,128)(2,1)S(1)} %bitcast.194), kind=kOutput, calls=%fused_computation.115 | convolution fusion | flops 637009920 | bytes 9724928 | tf_op jit(solution)/shard_map/bhwi,bhwo->io/dot_general | solution.py:23
  135.9 5.1 %fusion.116 = f32[1,128,128]{2,1,0:T(8,128)S(1)} fusion(bf16[2,50,1,128]{3,2,1,0:T(2,128)(2,1)S(1)} %collective-permute-done.2, bf16[2,50,192,128]{3,2,1,0:T(8,128)(2,1)S(1)} %bitcast.190, bf16[2,48,192,128]{3,2,1,0:T(8,128)(2,1)S(1)} %bitcast.194), kind=kOutput, calls=%fused_computation.116 | convolution fusion | flops 637009920 | bytes 9724928 | tf_op jit(solution)/shard_map/bhwi,bhwo->io/dot_general | solution.py:23
  142.0 4.2 %collective-permute-start.6 = (bf16[2,50,1,128]{3,2,1,0:T(2,128)(2,1)S(1)}, bf16[2,50,1,128]{3,2,1,0:T(2,128)(2,1)S(1)}, u32[]{:S(2)}, u32[]{:S(2)}) collective-permute-start(bf16[2,50,1,128]{3,2,1,0:T(2,128)(2,1)S(1)} %get-tuple-element.13), channel_id=1, source_target_pairs={{0,4},{4,8},{8,12},{12,16},{16,20},{20,24},{24,28},{1,5},{5,9},{9,... | collective-permute-start | bytes 76808 | tf_op jit(solution)/shard_map/ppermute | solution.py:40
  146.2 1.3 collective-permute-start.7
  147.5 1.5 fusion.104
  149.0 1.5 fusion.101
  150.5 1.7 collective-permute-done.7
  152.2 5.2 %pad_maximum_fusion = (bf16[2,50,193,128]{3,2,1,0:T(8,128)(2,1)S(1)}, bf16[2,50,193,128]{3,2,1,0:T(8,128)(2,1)S(1)}) fusion(bf16[2,50,1,128]{3,2,1,0:T(2,128)(2,1)S(1)} %collective-permute-done.7, bf16[2,1,192,128]{3,2,1,0:T(8,128)(2,1)S(1)} %collective-permute-done.5, bf16[2,48,192,128]{3,2,1,0:T(8,128)(2,1)S(1)} %fusion.9, ...), kind=kLoop, calls=%fused_computation.47 | loop fusion | flops 39526400 | bytes 14848000 | tf_op jit(solution)/shard_map/concatenate | solution.py:42
  157.3 1.6 fusion.79
  159.0 1.6 fusion.85
  160.6 1.5 fusion.82
  162.1 1.5 fusion.88
  163.6 1.6 fusion.91
  165.2 1.5 fusion.94
  166.8 6.5 %maximum_bitcast_fusion.1 = bf16[50,2,194,128]{3,2,0,1:T(8,128)(2,1)} fusion(bf16[2,50,1,128]{3,2,1,0:T(2,128)(2,1)S(1)} %collective-permute-done.7, bf16[2,1,192,128]{3,2,1,0:T(8,128)(2,1)S(1)} %collective-permute-done.5, bf16[2,48,192,128]{3,2,1,0:T(8,128)(2,1)S(1)} %fusion.9, bf16[2,1,192,128]{3,2,1,0:T(8,128)(2,1)S(1)} %collective-permute-done.4, ...), kind=kLoop, calls=%fused_computation.46 | loop fusion | flops 24832000 | bytes 9932800 | tf_op jit(solution)/shard_map/concatenate | solution.py:42
  173.3 8.5 %copy.43 = bf16[50,2,194,128]{3,1,2,0:T(2,128)(2,1)} copy(bf16[50,2,194,128]{3,2,0,1:T(8,128)(2,1)} %maximum_bitcast_fusion.1) | data formatting | bytes 9932800
  181.8 8.6 %pad.2.clone = bf16[50,2,200,128]{3,1,2,0:T(2,128)(2,1)} pad(bf16[50,2,194,128]{3,1,2,0:T(2,128)(2,1)} %copy.43, bf16[]{:T(256)} %constant.10), padding=0_0x0_0x0_6x0_0 | pad | bytes 10086402 | tf_op jit(solution)/shard_map/concatenate | solution.py:42
  191.7 6.8 %fusion.20 = bf16[50,2,8,27,128]{4,1,3,2,0:T(2,128)(2,1)S(1)} fusion(bf16[50,2,7,2,128]{4,1,3,2,0:T(2,128)(2,1)S(1)} %slice.122, bf16[50,2,8,25,128]{4,1,3,2,0:T(2,128)(2,1)} %bitcast.182), kind=kLoop, calls=%fused_computation.38 | loop fusion | flops 16588800 | bytes 11008000 | tf_op jit(solution)/shard_map/conv_general_dilated | solution.py:17
  198.5 12.2 %broadcast_select_fusion = f32[48,16,25,128]{3,1,2,0:T(8,128)S(1)} fusion(pred[16,25]{0,1:T(8,128)(4,1)S(1)} %copy-done.4, bf16[3,3,128,128]{3,2,1,0:T(8,128)(2,1)S(1)} %copy-done.3, bf16[50,2,8,27,128]{4,1,3,2,0:T(2,128)(2,1)S(1)} %fusion.20), kind=kOutput, calls=%fused_computation.49 | convolution fusion | flops 5664768000 | bytes 15655312 | tf_op jit(solution)/shard_map/conv_general_dilated | solution.py:17
  210.7 6.8 %copy.19 = f32[48,16,25,128]{3,0,2,1:T(8,128)} copy(f32[48,16,25,128]{3,1,2,0:T(8,128)S(1)} %broadcast_select_fusion) | data formatting | bytes 19660800 | tf_op jit(solution)/shard_map/conv_general_dilated | solution.py:17
  218.4 8.2 %fusion.18 = bf16[2,48,192,128]{3,1,2,0:T(8,128)(2,1)S(1)} fusion(f32[48,2,200,128]{3,0,2,1:T(8,128)} %bitcast.179, bf16[2,48,192,128]{3,2,1,0:T(8,128)(2,1)} %param.7), kind=kLoop, calls=%fused_computation.31 | loop fusion | flops 7077888 | bytes 18874368 | tf_op jit(solution)/shard_map/convert_element_type | solution.py:52
  226.6 3.4 copy.21
  230.1 121.6 %all-reduce.3.cloned.1.call-done = (f32[3,3,128,128]{2,3,1,0:T(8,128)}, f32[3,3,128,128]{3,2,1,0:T(8,128)}) async-done(((f32[3,3,128,128]{2,3,1,0:T(8,128)}, f32[3,3,128,128]{3,2,1,0:T(8,128)}), (f32[3,3,128,128]{2,3,1,0:T(8,128)}, f32[3,3,128,128]{3,2,1,0:T(8,128)})) %all-reduce.3.cloned.1.call-update) | async-done | bytes 1179664 | tf_op jit(solution)/shard_map/psum | solution.py:54
  351.6 2.1 copy.22
  353.7 1.9 copy.64
  (58 shorter events, 5.1 us)
Async XLA Ops:
  7.2 59.4 %copy-start = (bf16[3,3,128,128]{3,2,1,0:T(8,128)(2,1)S(1)}, bf16[3,3,128,128]{3,2,1,0:T(8,128)(2,1)}, u32[]{:S(2)}) copy-start(bf16[3,3,128,128]{3,2,1,0:T(8,128)(2,1)} %param.9) | copy-start | bytes 884740
  7.2 344.4 %all-reduce.3.cloned.1.call-start = ((), (), s32[]{:S(2)}) async-start(), calls=%async_computation | async-start | bytes 2359296 | tf_op jit(solution)/shard_map/psum | solution.py:54
  8.2 11.5 %collective-permute-start = (bf16[2,1,192,128]{3,2,1,0:T(8,128)(2,1)S(1)}, bf16[2,1,192,128]{3,2,1,0:T(8,128)(2,1)S(1)}, u32[]{:S(2)}, u32[]{:S(2)}) collective-permute-start(bf16[2,1,192,128]{3,2,1,0:T(8,128)(2,1)S(1)} %get-tuple-element.20), channel_id=1, source_target_pairs={{0,1},{1,2},{2,3},{4,5},{5,6},{6,7},{8,9},{9,10},{10,11},{12,13},{... | collective-permute-start | bytes 294920 | tf_op jit(solution)/shard_map/ppermute | solution.py:37
  10.7 9.1 %slice-start = ((s8[4718592]{0:T(1024)(128)(4,1)}), s8[4194304]{0:T(1024)(128)(4,1)S(1)}, s32[]{:S(2)}) async-start(s8[4718592]{0:T(1024)(128)(4,1)} %bitcast.185), calls=%async_computation.1 | async-start | bytes 8388608
  10.7 9.1 %slice-start.1 = ((s8[4718592]{0:T(1024)(128)(4,1)}), s8[524288]{0:T(1024)(128)(4,1)S(1)}, s32[]{:S(2)}) async-start(s8[4718592]{0:T(1024)(128)(4,1)} %bitcast.185), calls=%async_computation.2 | async-start | bytes 1048576
  10.7 9.8 %collective-permute-start.1 = (bf16[2,1,192,128]{3,2,1,0:T(8,128)(2,1)S(1)}, bf16[2,1,192,128]{3,2,1,0:T(8,128)(2,1)S(1)}, u32[]{:S(2)}, u32[]{:S(2)}) collective-permute-start(bf16[2,1,192,128]{3,2,1,0:T(8,128)(2,1)S(1)} %get-tuple-element.19), channel_id=1, source_target_pairs={{1,0},{2,1},{3,2},{5,4},{6,5},{7,6},{9,8},{10,9},{11,10},{13,12},{... | collective-permute-start | bytes 294920 | tf_op jit(solution)/shard_map/ppermute | solution.py:38
  19.7 7.6 %slice-start.6 = ((s8[4718592]{0:T(1024)(128)(4,1)}), s8[4194304]{0:T(1024)(128)(4,1)S(1)}, s32[]{:S(2)}) async-start(s8[4718592]{0:T(1024)(128)(4,1)} %bitcast.191), calls=%async_computation.7 | async-start | bytes 8388608
  19.8 7.6 %slice-start.7 = ((s8[4718592]{0:T(1024)(128)(4,1)}), s8[524288]{0:T(1024)(128)(4,1)S(1)}, s32[]{:S(2)}) async-start(s8[4718592]{0:T(1024)(128)(4,1)} %bitcast.191), calls=%async_computation.8 | async-start | bytes 1048576
  20.5 14.9 %copy-start.2 = (bf16[2,50,192,128]{3,2,1,0:T(8,128)(2,1)}, bf16[2,50,192,128]{3,2,1,0:T(8,128)(2,1)S(1)}, u32[]{:S(2)}) copy-start(bf16[2,50,192,128]{3,2,1,0:T(8,128)(2,1)S(1)} %constant_dynamic-update-slice_fusion) | copy-start | bytes 14745604
  20.6 14.8 %collective-permute-start.3 = (bf16[2,50,1,128]{3,2,1,0:T(2,128)(2,1)S(1)}, bf16[2,50,1,128]{3,2,1,0:T(2,128)(2,1)S(1)}, u32[]{:S(2)}, u32[]{:S(2)}) collective-permute-start(bf16[2,50,1,128]{3,2,1,0:T(2,128)(2,1)S(1)} %get-tuple-element.16), channel_id=1, source_target_pairs={{4,0},{8,4},{12,8},{16,12},{20,16},{24,20},{28,24},{5,1},{9,5},{13... | collective-permute-start | bytes 76808 | tf_op jit(solution)/shard_map/ppermute | solution.py:41
  22.2 13.2 %collective-permute-start.2 = (bf16[2,50,1,128]{3,2,1,0:T(2,128)(2,1)S(1)}, bf16[2,50,1,128]{3,2,1,0:T(2,128)(2,1)S(1)}, u32[]{:S(2)}, u32[]{:S(2)}) collective-permute-start(bf16[2,50,1,128]{3,2,1,0:T(2,128)(2,1)S(1)} %get-tuple-element.15), channel_id=1, source_target_pairs={{0,4},{4,8},{8,12},{12,16},{16,20},{20,24},{24,28},{1,5},{5,9},{9,... | collective-permute-start | bytes 76808 | tf_op jit(solution)/shard_map/ppermute | solution.py:40
  59.5 7.0 %copy-start.4 = (pred[16,25]{0,1:T(8,128)(4,1)S(1)}, pred[16,25]{0,1:T(8,128)(4,1)}, u32[]{:S(2)}) copy-start(pred[16,25]{0,1:T(8,128)(4,1)} %constant.18) | copy-start | bytes 1204
  59.6 32.4 %slice-start.8 = ((s8[4718592]{0:T(1024)(128)(4,1)}), s8[4194304]{0:T(1024)(128)(4,1)S(1)}, s32[]{:S(2)}) async-start(s8[4718592]{0:T(1024)(128)(4,1)} %bitcast.193), calls=%async_computation.9 | async-start | bytes 8388608
  66.5 25.4 %slice-start.9 = ((s8[4718592]{0:T(1024)(128)(4,1)}), s8[524288]{0:T(1024)(128)(4,1)S(1)}, s32[]{:S(2)}) async-start(s8[4718592]{0:T(1024)(128)(4,1)} %bitcast.193), calls=%async_computation.10 | async-start | bytes 1048576
  87.7 20.6 %slice-start.2 = ((s8[4718592]{0:T(1024)(128)(4,1)}), s8[524288]{0:T(1024)(128)(4,1)S(1)}, s32[]{:S(2)}) async-start(s8[4718592]{0:T(1024)(128)(4,1)} %bitcast.187), calls=%async_computation.3 | async-start | bytes 1048576
  91.9 16.3 %slice-start.3 = ((s8[4718592]{0:T(1024)(128)(4,1)}), s8[4194304]{0:T(1024)(128)(4,1)S(1)}, s32[]{:S(2)}) async-start(s8[4718592]{0:T(1024)(128)(4,1)} %bitcast.187), calls=%async_computation.4 | async-start | bytes 8388608
  101.6 40.3 %collective-permute-start.5 = (bf16[2,1,192,128]{3,2,1,0:T(8,128)(2,1)S(1)}, bf16[2,1,192,128]{3,2,1,0:T(8,128)(2,1)S(1)}, u32[]{:S(2)}, u32[]{:S(2)}) collective-permute-start(bf16[2,1,192,128]{3,2,1,0:T(8,128)(2,1)S(1)} %get-tuple-element.18), channel_id=1, source_target_pairs={{1,0},{2,1},{3,2},{5,4},{6,5},{7,6},{9,8},{10,9},{11,10},{13,12},{... | collective-permute-start | bytes 294920 | tf_op jit(solution)/shard_map/ppermute | solution.py:38
  102.9 6.9 %slice-start.4 = ((s8[4915200]{0:T(1024)(128)(4,1)}), s8[4194304]{0:T(1024)(128)(4,1)S(1)}, s32[]{:S(2)}) async-start(s8[4915200]{0:T(1024)(128)(4,1)} %bitcast.189), calls=%async_computation.5 | async-start | bytes 8388608
  102.9 6.9 %slice-start.5 = ((s8[4915200]{0:T(1024)(128)(4,1)}), s8[720896]{0:T(1024)(128)(4,1)S(1)}, s32[]{:S(2)}) async-start(s8[4915200]{0:T(1024)(128)(4,1)} %bitcast.189), calls=%async_computation.6 | async-start | bytes 1441792
  102.9 39.0 %collective-permute-start.4 = (bf16[2,1,192,128]{3,2,1,0:T(8,128)(2,1)S(1)}, bf16[2,1,192,128]{3,2,1,0:T(8,128)(2,1)S(1)}, u32[]{:S(2)}, u32[]{:S(2)}) collective-permute-start(bf16[2,1,192,128]{3,2,1,0:T(8,128)(2,1)S(1)} %get-tuple-element.17), channel_id=1, source_target_pairs={{0,1},{1,2},{2,3},{4,5},{5,6},{6,7},{8,9},{9,10},{10,11},{12,13},{... | collective-permute-start | bytes 294920 | tf_op jit(solution)/shard_map/ppermute | solution.py:37
  142.0 8.5 %collective-permute-start.6 = (bf16[2,50,1,128]{3,2,1,0:T(2,128)(2,1)S(1)}, bf16[2,50,1,128]{3,2,1,0:T(2,128)(2,1)S(1)}, u32[]{:S(2)}, u32[]{:S(2)}) collective-permute-start(bf16[2,50,1,128]{3,2,1,0:T(2,128)(2,1)S(1)} %get-tuple-element.13), channel_id=1, source_target_pairs={{0,4},{4,8},{8,12},{12,16},{16,20},{20,24},{24,28},{1,5},{5,9},{9,... | collective-permute-start | bytes 76808 | tf_op jit(solution)/shard_map/ppermute | solution.py:40
  146.2 6.0 %collective-permute-start.7 = (bf16[2,50,1,128]{3,2,1,0:T(2,128)(2,1)S(1)}, bf16[2,50,1,128]{3,2,1,0:T(2,128)(2,1)S(1)}, u32[]{:S(2)}, u32[]{:S(2)}) collective-permute-start(bf16[2,50,1,128]{3,2,1,0:T(2,128)(2,1)S(1)} %get-tuple-element.14), channel_id=1, source_target_pairs={{4,0},{8,4},{12,8},{16,12},{20,16},{24,20},{28,24},{5,1},{9,5},{13... | collective-permute-start | bytes 76808 | tf_op jit(solution)/shard_map/ppermute | solution.py:41
  191.7 6.8 %copy-start.3 = (bf16[3,3,128,128]{3,2,1,0:T(8,128)(2,1)S(1)}, bf16[3,3,128,128]{3,2,1,0:T(8,128)(2,1)}, u32[]{:S(2)}) copy-start(bf16[3,3,128,128]{3,2,1,0:T(8,128)(2,1)} %param.8) | copy-start | bytes 884740
  218.4 137.3 %copy-start.1 = (bf16[3,3,128,128]{3,2,1,0:T(8,128)(2,1)S(1)}, bf16[3,3,128,128]{3,2,1,0:T(8,128)(2,1)}, u32[]{:S(2)}) copy-start(bf16[3,3,128,128]{3,2,1,0:T(8,128)(2,1)} %param.9) | copy-start | bytes 884740
Sparse Core Ops, SparseCore 0:
  218.5 133.0 all-reduce.2
where the time goes:
time: 368 us; the launch traced here: 363 us
  waiting for transfers between devices  123 us (33%)
  matrix products  86.9 us (24%)
  local copies, waits for them, and re-layouts  64.2 us (17%)
  other arithmetic  50.6 us (14%)
  starting transfers between devices  22.9 us (6%)
  between operations  14.8 us (4%)
    psum x1, waiting for transfers between devices, local_step(): d_w1, d_w2 = lax.psum((w1_part, w2_part), ('row', 'col'))  122 us
    dot_general x18, matrix products, tap_grads(): jnp.einsum('bhwi,bhwo->io', tile_in, grad_wide[:, 2 - tap_row:2 - tap_row...  60.5 us
    conv_general_dilated x2, matrix products, conv_valid(): lax.conv_general_dilated(lhs_arr, rhs_arr, (1, 1), 'VALID', dimension_num...  26.4 us
    unnamed x37, local copies, waits for them, and re-layouts  25.5 us
    conv_general_dilated x5, local copies, waits for them, and re-layouts, conv_valid(): lax.conv_general_dilated(lhs_arr, rhs_arr, (1, 1), 'VALID', dimension_num...  20.5 us
    concatenate x3, other arithmetic, add_halo(): return jnp.concatenate([from_left, tall, from_right], axis=2)  17.2 us
    concatenate x2, local copies, waits for them, and re-layouts, add_halo(): return jnp.concatenate([from_left, tall, from_right], axis=2)  17.1 us
    conv_general_dilated x2, other arithmetic, conv_valid(): lax.conv_general_dilated(lhs_arr, rhs_arr, (1, 1), 'VALID', dimension_num...  13.7 us
  transfers between devices with their start and end apart: 9, of which 2 were waited for; matrix products, arithmetic and copies ran while one was open for 18% of the time, Pallas kernels for 0%

commit v1 on v0

v1 whole, which is shorter than its diff:
```python
import functools

import jax
import jax.numpy as jnp
from jax import lax
from jax.experimental import pallas as pl
from jax.experimental.pallas import tpu as pltpu
from jax.sharding import PartitionSpec as P

MESH = pl.DeviceIdType.MESH
F32 = jnp.float32
BF16 = jnp.bfloat16
IMGS = 2
ROWS = 48
COLS = 192
CH = 128
HALF = COLS // 2
G_ROWS = ROWS + 4
A_ROWS = ROWS + 2
TANH_SCALE = 0.7978845608028654
CUBE_COEF = 0.044715
A_STEP = 5
B_STEP = 8


def gelu_both(a_val):
    sq = a_val * a_val
    tanh_val = jnp.tanh(TANH_SCALE * (a_val + CUBE_COEF * sq * a_val))
    half = 0.5 * a_val
    plus = 1.0 + tanh_val
    slope = 0.5 * plus + half * (1.0 - tanh_val * tanh_val) * (TANH_SCALE + (TANH_SCALE * 3.0 * CUBE_COEF) * sq)
    return half * plus, slope


def halo_kernel(n_row, n_col, a_hbm, g_hbm, gn, gs, an, as_, rl, rr, cnw, cne, csw, cse,
                strip, wide, pack_l, pack_r, loc_sem, send_sem, recv_sem):
    row = lax.axis_index("row")
    col = lax.axis_index("col")
    has_n, has_s = row > 0, row < n_row - 1
    has_w, has_e = col > 0, col < n_col - 1
    dirs = {
        "n": (has_n, row - 1, col), "s": (has_s, row + 1, col),
        "w": (has_w, row, col - 1), "e": (has_e, row, col + 1),
        "nw": (has_n & has_w, row - 1, col - 1), "ne": (has_n & has_e, row - 1, col + 1),
        "sw": (has_s & has_w, row + 1, col - 1), "se": (has_s & has_e, row + 1, col + 1),
    }
    barrier = pltpu.get_barrier_semaphore()
    locals_ = []
    for k, (src, c0) in enumerate(((g_hbm, 0), (g_hbm, COLS - 16), (a_hbm, 0), (a_hbm, COLS - 16))):
        cp = pltpu.make_async_copy(src.at[:, :, pl.ds(c0, 16), :], strip.at[k], loc_sem.at[k])
        cp.start()
        locals_.append(cp)
    for ok, r, c in dirs.values():
        @pl.when(ok)
        def _(r=r, c=c):
            pl.semaphore_signal(barrier, inc=1, device_id=(c, r), device_id_type=MESH)
    for ok, refs in ((has_n, (gn, an)), (has_s, (gs, as_)), (has_w, (rl,)), (has_e, (rr,)),
                     (dirs["nw"][0], (cnw,)), (dirs["ne"][0], (cne,)), (dirs["sw"][0], (csw,)), (dirs["se"][0], (cse,))):
        @pl.when(jnp.logical_not(ok))
        def _(refs=refs):
            for ref in refs:
                ref[...] = jnp.zeros_like(ref)
    n_s, w_e = has_n.astype(jnp.int32) + has_s.astype(jnp.int32), has_w.astype(jnp.int32) + has_e.astype(jnp.int32)
    pl.semaphore_wait(barrier, n_s + w_e + n_s * w_e)

    def rcopy(k, src, dst, where):
        _, r, c = dirs[where]
        return pltpu.make_async_remote_copy(src_ref=src, dst_ref=dst, send_sem=send_sem.at[k], recv_sem=recv_sem.at[k],
                                            device_id=(c, r), device_id_type=MESH)

    copies = [
        ("s", "n", g_hbm.at[:, pl.ds(ROWS - 2, 2)], gn),
        ("n", "s", g_hbm.at[:, pl.ds(0, 2)], gs),
        ("s", "n", a_hbm.at[:, pl.ds(ROWS - 1, 1)], an),
        ("n", "s", a_hbm.at[:, pl.ds(0, 1)], as_),
        ("e", "w", pack_r, rl),
        ("w", "e", pack_l, rr),
        ("se", "nw", pack_r.at[:, :, pl.ds(32, 16)], cnw),
        ("sw", "ne", pack_l.at[:, :, pl.ds(32, 16)], cne),
        ("ne", "sw", pack_r.at[:, :, pl.ds(0, 16)], csw),
        ("nw", "se", pack_l.at[:, :, pl.ds(0, 16)], cse),
    ]

    def start(k):
        to, _, src, dst = copies[k]
        @pl.when(dirs[to][0])
        def _():
            rcopy(k, src, dst, to).start()

    for k in range(4):
        start(k)
    for k in range(4):
        locals_[k].wait()
        base = 0 if k % 2 == 0 else 8
        for m in range(IMGS):
            wide[...] = strip[k, m].astype(F32).reshape(ROWS * 16, CH)
            pack = pack_l if k % 2 == 0 else pack_r
            if k < 2:
                first = 0 if k == 0 else 14
                pack[m, 0] = wide[pl.ds(first, ROWS, stride=16), :].astype(BF16)
                pack[m, 1] = wide[pl.ds(first + 1, ROWS, stride=16), :].astype(BF16)
            else:
                pack[m, 2] = wide[pl.ds(0 if k == 2 else 15, ROWS, stride=16), :].astype(BF16)
    for k in range(4, 10):
        start(k)
    for k in range(10):
        to, frm, src, dst = copies[k]
        @pl.when(dirs[to][0])
        def _():
            rcopy(k, src, dst, to).wait_send()
        @pl.when(dirs[frm][0])
        def _():
            rcopy(k, src, dst, frm).wait_recv()


def halo(mesh_shape, a_tile, g_tile):
    vm = pl.BlockSpec(memory_space=pltpu.VMEM)
    outs = [((IMGS, 2, COLS, CH)), ((IMGS, 2, COLS, CH)), ((IMGS, 1, COLS, CH)), ((IMGS, 1, COLS, CH)),
            (IMGS, 3, ROWS, CH), (IMGS, 3, ROWS, CH)] + [(IMGS, 3, 16, CH)] * 4
    return pl.pallas_call(
        functools.partial(halo_kernel, mesh_shape["row"], mesh_shape["col"]),
        out_shape=[jax.ShapeDtypeStruct(s, BF16) for s in outs],
        in_specs=[pl.BlockSpec(memory_space=pl.ANY)] * 2,
        out_specs=[vm] * len(outs),
        scratch_shapes=[
            pltpu.VMEM((4, IMGS, ROWS, 16, CH), BF16),
            pltpu.VMEM((ROWS * 16, CH), F32),
            pltpu.VMEM((IMGS, 3, ROWS, CH), BF16),
            pltpu.VMEM((IMGS, 3, ROWS, CH), BF16),
            pltpu.SemaphoreType.DMA((4,)),
            pltpu.SemaphoreType.DMA((10,)),
            pltpu.SemaphoreType.DMA((10,)),
        ],
        compiler_params=pltpu.CompilerParams(collective_id=0, has_side_effects=True),
        name="halo",
    )(a_tile, g_tile)


def compute_kernel(n_row, n_col, x_hbm, a_hbm, g_hbm, gn, gs, an, as_, rl, rr, cnw, cne, csw, cse, w1, w2,
                   dx_hbm, dw,
                   g_buf, a_buf, x_buf, g4, d4, zp, band1, band2, w9, acc1, acc2, dz_ref,
                   s_g, s_a, s_e, s_o, gcol, acol, dcol, o_st,
                   in_sem, out_sem):
    row = lax.axis_index("row")
    col = lax.axis_index("col")
    loads = {}
    for m in range(IMGS):
        for j, (src, dst) in enumerate((
            (g_hbm.at[m], g_buf.at[m, pl.ds(2, ROWS)]), (gn.at[m], g_buf.at[m, pl.ds(0, 2)]), (gs.at[m], g_buf.at[m, pl.ds(ROWS + 2, 2)]),
            (a_hbm.at[m], a_buf.at[m, pl.ds(1, ROWS)]), (an.at[m], a_buf.at[m, pl.ds(0, 1)]), (as_.at[m], a_buf.at[m, pl.ds(ROWS + 1, 1)]),
            (x_hbm.at[m], x_buf.at[m]),
        )):
            loads[m, j] = pltpu.make_async_copy(src, dst, in_sem.at[m, j])
    for j in range(7):
        for m in range(IMGS):
            loads[m, j].start()

    for w, band in ((w1, band1), (w2, band2)):
        for dri in range(3):
            band[pl.ds(dri * 512 + 384, CH), pl.ds(0, CH)] = jnp.zeros((CH, CH), BF16)
            band[pl.ds(dri * 512, CH), pl.ds(CH, CH)] = jnp.zeros((CH, CH), BF16)
        for a in range(3):
            for c in range(3):
                tap = w[a, c].astype(F32).T.astype(BF16)
                dri = 2 - a
                band[pl.ds(dri * 512 + (2 - c) * CH, CH), pl.ds(0, CH)] = tap
                band[pl.ds(dri * 512 + (3 - c) * CH, CH), pl.ds(CH, CH)] = tap
                if w is w2:
                    w9[pl.ds((dri * 3 + 2 - c) * CH, CH), :] = tap
    acc1[...] = jnp.zeros_like(acc1)
    acc2[...] = jnp.zeros_like(acc2)

    for side, (mid, top, bot) in enumerate(((rl, cnw, csw), (rr, cne, cse))):
        for m in range(IMGS):
            for k in range(2):
                slot = k if side == 0 else k + 1
                gcol[side, m, slot, pl.ds(8, ROWS), :] = mid[m, k].astype(F32)
                gcol[side, m, slot, pl.ds(6, 2), :] = top[m, k].astype(F32)[14:16]
                gcol[side, m, slot, pl.ds(8 + ROWS, 2), :] = bot[m, k].astype(F32)[0:2]
            acol[side, m, pl.ds(8, ROWS), :] = mid[m, 2].astype(F32)
            acol[side, m, pl.ds(7, 1), :] = top[m, 2].astype(F32)[15:16]
            acol[side, m, pl.ds(8 + ROWS, 1), :] = bot[m, 2].astype(F32)[0:1]
    for m in range(IMGS):
        for j in range(3):
            loads[m, j].wait()
    for m in range(IMGS):
        for side in range(2):
            edge = g_buf[m, :, pl.ds(0 if side == 0 else COLS - 16, 16), :].astype(F32)
            s_g[pl.ds(0, G_ROWS * 16), :] = edge.reshape(G_ROWS * 16, CH)
            gcol[side, m, 2 if side == 0 else 0, pl.ds(6, G_ROWS), :] = s_g[pl.ds(0 if side == 0 else 15, G_ROWS, stride=16), :]
    for m in range(IMGS):
        for j in range(3, 7):
            loads[m, j].wait()
    for side in range(2):
        inside = (col > 0) if side == 0 else (col < n_col - 1)
        for m in range(IMGS):
            lhs = jnp.concatenate(
                [gcol[side, m, dci, pl.ds(6 + dri, 56), :].astype(BF16) for dri in range(3) for dci in range(3)], axis=1)
            dz_col = jnp.dot(lhs, w9[...], preferred_element_type=F32)
            _, slope = gelu_both(acol[side, m, pl.ds(7, 56), :])
            dcol[side, m] = jnp.where(inside, dz_col * slope, 0.0)

    def build_g4(n, carry):
        m, r0 = n // 13, (n % 13) * 4
        for t in range(4):
            base = t * 208
            s_g[pl.ds(base + 8, COLS), :] = g_buf[m, r0 + t].astype(F32)
            s_g[pl.ds(base + 7, 1), :] = gcol[0, m, 1, pl.ds(6 + r0 + t, 1), :]
            s_g[pl.ds(base + 8 + COLS, 1), :] = gcol[1, m, 1, pl.ds(6 + r0 + t, 1), :]
            at = pl.multiple_of((m * G_ROWS + r0 + t) * HALF, 32)
            for q in range(4):
                g4[pl.ds(at, HALF), pl.ds(q * CH, CH)] = s_g[pl.ds(base + 7 + q, HALF, stride=2), :].astype(BF16)
        return carry

    lax.fori_loop(0, 2 * 13, build_g4, 0)

    def conv_a(n):
        m, d0 = n // 10, (n % 10) * A_STEP
        lhs = jnp.concatenate(
            [g4[pl.ds(pl.multiple_of((m * G_ROWS + d0 + t) * HALF, 32), A_STEP * HALF), :] for t in range(3)], axis=1)
        return jnp.dot(lhs, band2[...], preferred_element_type=F32)

    dz_ref[...] = conv_a(0)

    def step_a(n, carry):
        m, d0 = n // 10, (n % 10) * A_STEP
        for t in range(A_STEP):
            base = t * COLS
            s_a[pl.ds(base, COLS), :] = a_buf[m, d0 + t].astype(F32)
            at = pl.multiple_of((m * A_ROWS + d0 + t) * HALF, 32)
            z_e, slope_e = gelu_both(s_a[pl.ds(base, HALF, stride=2), :])
            z_o, slope_o = gelu_both(s_a[pl.ds(base + 1, HALF, stride=2), :])
            zp[pl.ds(at, HALF), pl.ds(0, CH)] = z_e.astype(BF16)
            zp[pl.ds(at, HALF), pl.ds(CH, CH)] = z_o.astype(BF16)
            da_e = dz_ref[pl.ds(t * HALF, HALF), pl.ds(0, CH)] * slope_e
            da_o = dz_ref[pl.ds(t * HALF, HALF), pl.ds(CH, CH)] * slope_o
            s_e[t, pl.ds(8, HALF), :] = da_e
            s_o[t, pl.ds(8, HALF), :] = da_o
            s_o[t, pl.ds(7, 1), :] = dcol[0, m, pl.ds(d0 + t, 1), :]
            s_e[t, pl.ds(8 + HALF, 1), :] = dcol[1, m, pl.ds(d0 + t, 1), :]
            d4[pl.ds(at, HALF), pl.ds(0, CH)] = s_o[t, pl.ds(7, HALF), :].astype(BF16)
            d4[pl.ds(at, HALF), pl.ds(CH, CH)] = da_e.astype(BF16)
            d4[pl.ds(at, HALF), pl.ds(2 * CH, CH)] = da_o.astype(BF16)
            d4[pl.ds(at, HALF), pl.ds(3 * CH, CH)] = s_e[t, pl.ds(9, HALF), :].astype(BF16)
        dz_ref[...] = conv_a(jnp.minimum(n + 1, 19))
        return carry

    lax.fori_loop(0, 20, step_a, 0)
    for m in range(IMGS):
        for edge, ok in ((0, row > 0), (A_ROWS - 1, row < n_row - 1)):
            @pl.when(jnp.logical_not(ok))
            def _(m=m, edge=edge):
                d4[pl.ds((m * A_ROWS + edge) * HALF, HALF), :] = jnp.zeros((HALF, 4 * CH), BF16)

    def out_copy(n):
        m, r0 = n // 6, (n % 6) * B_STEP
        return pltpu.make_async_copy(o_st.at[n % 2], dx_hbm.at[m, pl.ds(r0, B_STEP)], out_sem.at[n % 2])

    def step_b(n, carry):
        m, r0 = n // 6, (n % 6) * B_STEP
        cnt = B_STEP * HALF
        z_chunk = zp[pl.ds(pl.multiple_of((m * A_ROWS + r0 + 1) * HALF, 32), cnt), :]
        g_win = jnp.concatenate(
            [g4[pl.ds(pl.multiple_of((m * G_ROWS + r0 + 1 + t) * HALF, 32), cnt), :] for t in range(3)], axis=1)
        acc2[...] += lax.dot_general(z_chunk, g_win, (((0,), (0,)), ((), ())), preferred_element_type=F32)
        xs = []
        for t in range(B_STEP):
            s_a[pl.ds(t * COLS, COLS), :] = x_buf[m, r0 + t].astype(F32)
        for t in range(B_STEP):
            xs.append(jnp.concatenate([s_a[pl.ds(t * COLS, HALF, stride=2), :].astype(BF16),
                                       s_a[pl.ds(t * COLS + 1, HALF, stride=2), :].astype(BF16)], axis=1))
        x_chunk = jnp.concatenate(xs, axis=0)
        d_win = jnp.concatenate(
            [d4[pl.ds(pl.multiple_of((m * A_ROWS + r0 + t) * HALF, 32), cnt), :] for t in range(3)], axis=1)
        acc1[...] += lax.dot_general(x_chunk, d_win, (((0,), (0,)), ((), ())), preferred_element_type=F32)
        dx = jnp.dot(d_win, band1[...], preferred_element_type=F32)
        g_own = g4[pl.ds(pl.multiple_of((m * G_ROWS + r0 + 2) * HALF, 32), cnt), pl.ds(CH, 2 * CH)].astype(F32)
        dx = dx + g_own

        @pl.when(n >= 2)
        def _():
            out_copy(n).wait()
        for t in range(B_STEP):
            s_g[pl.ds(t * COLS, HALF, stride=2), :] = dx[t * HALF:(t + 1) * HALF, :CH]
            s_g[pl.ds(t * COLS + 1, HALF, stride=2), :] = dx[t * HALF:(t + 1) * HALF, CH:]
        for t in range(B_STEP):
            o_st[n % 2, t] = s_g[pl.ds(t * COLS, COLS), :].astype(BF16)
        out_copy(n).start()
        return carry

    lax.fori_loop(0, 12, step_b, 0)
    for k, acc in enumerate((acc2, acc1)):
        for a in range(3):
            for c in range(3):
                at = (2 - a) * 512 + (2 - c) * CH
                dw[pl.ds((k * 9 + a * 3 + c) * CH, CH), :] = acc[pl.ds(0, CH), pl.ds(at, CH)] + acc[pl.ds(CH, CH), pl.ds(at + CH, CH)]
    out_copy(10).wait()
    out_copy(11).wait()


def compute(mesh_shape, x_tile, a_tile, g_tile, halos, w_one, w_two):
    vm = pl.BlockSpec(memory_space=pltpu.VMEM)
    hbm = pl.BlockSpec(memory_space=pl.ANY)
    return pl.pallas_call(
        functools.partial(compute_kernel, mesh_shape["row"], mesh_shape["col"]),
        out_shape=[jax.ShapeDtypeStruct((IMGS, ROWS, COLS, CH), BF16), jax.ShapeDtypeStruct((18 * CH, CH), F32)],
        in_specs=[hbm] * 7 + [vm] * 8,
        out_specs=[hbm, vm],
        scratch_shapes=[
            pltpu.VMEM((IMGS, G_ROWS, COLS, CH), BF16),
            pltpu.VMEM((IMGS, A_ROWS, COLS, CH), BF16),
            pltpu.VMEM((IMGS, ROWS, COLS, CH), BF16),
            pltpu.VMEM((IMGS * G_ROWS * HALF, 4 * CH), BF16),
            pltpu.VMEM((IMGS * A_ROWS * HALF, 4 * CH), BF16),
            pltpu.VMEM((IMGS * A_ROWS * HALF, 2 * CH), BF16),
            pltpu.VMEM((12 * CH, 2 * CH), BF16),
            pltpu.VMEM((12 * CH, 2 * CH), BF16),
            pltpu.VMEM((9 * CH, CH), BF16),
            pltpu.VMEM((2 * CH, 12 * CH), F32),
            pltpu.VMEM((2 * CH, 12 * CH), F32),
            pltpu.VMEM((A_STEP * HALF, 2 * CH), F32),
            pltpu.VMEM((B_STEP * COLS + 64, CH), F32),
            pltpu.VMEM((B_STEP * COLS, CH), F32),
            pltpu.VMEM((A_STEP, HALF + 16, CH), F32),
            pltpu.VMEM((A_STEP, HALF + 16, CH), F32),
            pltpu.VMEM((2, IMGS, 3, 72, CH), F32),
            pltpu.VMEM((2, IMGS, 72, CH), F32),
            pltpu.VMEM((2, IMGS, 56, CH), F32),
            pltpu.VMEM((2, B_STEP, COLS, CH), BF16),
            pltpu.SemaphoreType.DMA((IMGS, 7)),
            pltpu.SemaphoreType.DMA((2,)),
        ],
        compiler_params=pltpu.CompilerParams(vmem_limit_bytes=67043328),
        name="block_grads",
    )(x_tile, a_tile, g_tile, *halos, w_one, w_two)


CHAINS = ((0, 1024), (1024, 1280))


def sum_kernel(part, out1, out2, data, full, bufs0, bufs1, in_sem, send_sem, recv_sem):
    row, col = lax.axis_index("row"), lax.axis_index("col")
    x, core, z, y = row // 2, row % 2, col // 2, col % 2
    load = pltpu.make_async_copy(part, data, in_sem.at[0])
    load.start()
    x_peer = (col, 2 * (1 - x) + core)
    y_peer = (2 * z + 1 - y, row)
    core_peer = (col, 2 * x + 1 - core)
    z_peers = [(2 * ((z + t) % 4) + y, row) for t in (1, 2, 3)]
    barrier = pltpu.get_barrier_semaphore()
    for peer in (x_peer, y_peer, core_peer, *z_peers):
        pl.semaphore_signal(barrier, inc=1, device_id=peer, device_id_type=MESH)
    pl.semaphore_wait(barrier, 6)
    load.wait()
    first = (jnp.where(core == 0, col, y_peer[0]), jnp.where(core == 0, x_peer[1], row))
    second = (jnp.where(core == 0, y_peer[0], col), jnp.where(core == 0, row, x_peer[1]))
    bit1 = jnp.where(core == 0, x, y)
    bit2 = jnp.where(core == 0, y, x)
    sends = []

    def remote(src, dst, sem, peer):
        copy = pltpu.make_async_remote_copy(src_ref=src, dst_ref=dst, send_sem=send_sem.at[sem], recv_sem=recv_sem.at[sem],
                                            device_id=peer, device_id_type=MESH)
        return copy

    def rows(ref, at, count):
        return ref.at[pl.ds(pl.multiple_of(at, 8), count)]

    def chain(k):
        base, size = CHAINS[k]
        bufs = (bufs0, bufs1)[k]
        sem = 12 * k
        at = base
        buf_at = 0
        keep = base
        for stage, (bit, peer) in enumerate(((core, core_peer), (bit1, first), (bit2, second))):
            part_size = size >> (stage + 1)
            keep = at + bit * part_size
            copy = remote(rows(data, at + (1 - bit) * part_size, part_size), bufs.at[pl.ds(buf_at, part_size)], sem + stage, peer)
            copy.start()
            sends.append(copy)
            yield
            copy.wait_recv()
            mine = pl.ds(pl.multiple_of(keep, 8), part_size)
            data[mine, :] = data[mine, :] + bufs[pl.ds(buf_at, part_size), :]
            at = keep
            buf_at += part_size
        quarter = size // 32
        copies = []
        for t in (1, 2, 3):
            copy = remote(rows(data, at + ((z + t) % 4) * quarter, quarter), bufs.at[pl.ds(buf_at + (3 - t) * quarter, quarter)],
                          sem + 2 + t, z_peers[t - 1])
            copy.start()
            copies.append(copy)
        sends.extend(copies)
        yield
        for copy in copies:
            copy.wait_recv()
        mine = pl.ds(pl.multiple_of(at + z * quarter, 8), quarter)
        total = data[mine, :]
        for t in range(3):
            total = total + bufs[pl.ds(buf_at + t * quarter, quarter), :]
        full[mine, :] = total
        copies = []
        for t in (1, 2, 3):
            piece = rows(full, at + z * quarter, quarter)
            copy = remote(piece, piece, sem + 5 + t, z_peers[t - 1])
            copy.start()
            copies.append(copy)
        sends.extend(copies)
        yield
        for copy in copies:
            copy.wait_recv()
        for stage, (bit, peer) in ((2, (bit2, second)), (1, (bit1, first)), (0, (core, core_peer))):
            part_size = size >> (stage + 1)
            piece = rows(full, at, part_size)
            copy = remote(piece, piece, sem + 9 + stage, peer)
            copy.start()
            sends.append(copy)
            yield
            copy.wait_recv()
            at = at - bit * part_size

    running = [chain(0), chain(1)]
    while running:
        for one in list(running):
            try:
                next(one)
            except StopIteration:
                running.remove(one)
    for copy in sends:
        copy.wait_send()
    outs = [pltpu.make_async_copy(full.at[pl.ds(k * 9 * CH, 9 * CH)], (out2, out1)[k], in_sem.at[k]) for k in range(2)]
    for copy in outs:
        copy.start()
    for copy in outs:
        copy.wait()


def device_sum(part):
    hbm = pl.BlockSpec(memory_space=pl.ANY)
    return pl.pallas_call(
        sum_kernel,
        out_shape=[jax.ShapeDtypeStruct((9 * CH, CH), F32)] * 2,
        in_specs=[hbm],
        out_specs=[hbm] * 2,
        scratch_shapes=[
            pltpu.VMEM((18 * CH, CH), F32),
            pltpu.VMEM((18 * CH, CH), F32),
            pltpu.VMEM((1024, CH), F32),
            pltpu.VMEM((1280, CH), F32),
            pltpu.SemaphoreType.DMA((2,)),
            pltpu.SemaphoreType.DMA((24,)),
            pltpu.SemaphoreType.DMA((24,)),
        ],
        compiler_params=pltpu.CompilerParams(collective_id=1, has_side_effects=True),
        name="device_sum",
    )(part)


def solution(mesh):
    shape = dict(mesh.shape)

    def local_step(x_tile, a_tile, g_tile, w_one, w_two):
        halos = halo(shape, a_tile, g_tile)
        d_x, dw = compute(shape, x_tile, a_tile, g_tile, halos, w_one, w_two)
        d_w1, d_w2 = device_sum(dw)
        return d_x, d_w1.reshape(3, 3, CH, CH), d_w2.reshape(3, 3, CH, CH)

    tile_spec = P(None, "row", "col", None)
    return jax.shard_map(local_step, mesh=mesh, in_specs=(tile_spec, tile_spec, tile_spec, P(), P()), out_specs=(tile_spec, P(), P()), check_vma=False)
```

time: 368 us -> 105 us (0.29); the launches traced: 363 us -> 105 us
  waiting for transfers between devices: 123 us -> 0 us
  Pallas kernels: 0 us -> 100 us
  matrix products: 86.9 us -> 0 us
  local copies, waits for them, and re-layouts: 64.2 us -> 3.83 us
  other arithmetic: 50.6 us -> 0 us
  starting transfers between devices: 22.9 us -> 0 us
  between operations: 14.8 us -> 0.65 us
    psum x1 -> x0, waiting for transfers between devices: 122 us -> none  [local_step(): d_w1, d_w2 = lax.psum((w1_part, w2_part), ('row', 'col'))]
    pallas_call x0 -> x3, Pallas kernels: none -> 100 us  [the longest x1 55.7 us: compute(): pl.pallas_call(functools.partial(compute_kernel, mesh_shape['row'], mesh_...]
    dot_general x18 -> x0, matrix products: 60.5 us -> none  [tap_grads(): jnp.einsum('bhwi,bhwo->io', tile_in, grad_wide[:, 2 - tap_row:2 - tap_row...]
    conv_general_dilated x2 -> x0, matrix products: 26.4 us -> none  [conv_valid(): lax.conv_general_dilated(lhs_arr, rhs_arr, (1, 1), 'VALID', dimension_num...]
    ppermute x8 -> x0, starting transfers between devices: 22.8 us -> none  [the longest x2 9.38 us: add_halo(): from_left = lax.ppermute(tall[:, :, -1:], 'col', col_down)]
    unnamed x37 -> x2, local copies, waits for them, and re-layouts: 25.5 us -> 3.83 us
    conv_general_dilated x5 -> x0, local copies, waits for them, and re-layouts: 20.5 us -> none  [conv_valid(): lax.conv_general_dilated(lhs_arr, rhs_arr, (1, 1), 'VALID', dimension_num...]
    convert_element_type x2 -> x0, other arithmetic: 17.8 us -> none  [the longest x1 9.6 us: local_step(): d_a = (d_z * gelu_slope(a_val)).astype(jnp.bfloat16)]
  transfers between devices with their start and end apart: 9 -> 0, of which waited for: 2 -> 0; matrix products, arithmetic and copies ran while one was open for 18% -> 0% of each run, Pallas kernels for 0% -> 0%
where the time goes in v1:
time: 105 us
  Pallas kernels  100 us (95%)
  local copies, waits for them, and re-layouts  3.83 us (4%)
    pallas_call x1, Pallas kernels, compute(): pl.pallas_call(functools.partial(compute_kernel, mesh_shape['row'], mesh_...  55.7 us
    pallas_call x1, Pallas kernels, device_sum(): pl.pallas_call(sum_kernel, out_shape=[jax.ShapeDtypeStruct((9 * CH, CH),...  34.9 us
    pallas_call x1, Pallas kernels, halo(): pl.pallas_call(functools.partial(halo_kernel, mesh_shape['row'], mesh_sha...  9.66 us
    unnamed x2, local copies, waits for them, and re-layouts  3.83 us

profile of v1, /device:TPU:0, one launch (start us, length us, event | category | flops | bytes accessed | tf_op | source)
XLA Modules:
  0.0 104.8 jit_solution(417994589674686948)
XLA Ops:
  0.6 9.7 %halo.1 = (bf16[2,2,192,128]{3,2,1,0:T(8,128)(2,1)}, bf16[2,2,192,128]{3,2,1,0:T(8,128)(2,1)}, bf16[2,1,192,128]{3,2,1,0:T(8,128)(2,1)}, bf16[2,1,192,128]{3,2,1...) custom-call(bf16[2,48,192,128]{3,2,1,0:T(8,128)(2,1)} %a_hbm.3, ...), custom_call_target="tpu_custom_call" | custom-call | tf_op jit(solution)/shard_map/halo/pallas_call | solution.py:120
  10.3 55.7 %block_grads.1 = (bf16[2,48,192,128]{3,2,1,0:T(8,128)(2,1)}, f32[2304,128]{1,0:T(8,128)}) custom-call(bf16[2,48,192,128]{3,2,1,0:T(8,128)(2,1)} %x_hbm.1, bf16[2,48,192,128]{3,2,1,0:T(8,128)(2,1)} %a_hbm.3, bf16[2,48,192,128]{3,2,1,0:T(8,128)(2,1)} %g_hbm.3, bf16[2,2,192,128]{3,2,1,0:T(8,128)(2,1)} %get-tuple-element.17.gn, ...), custom_call_target="tpu_custom_call" | custom-call | tf_op jit(solution)/shard_map/block_grads/pallas_call | solution.py:304
  66.0 34.9 %device_sum.1 = (f32[1152,128]{1,0:T(8,128)}, f32[1152,128]{1,0:T(8,128)}) custom-call(f32[2304,128]{1,0:T(8,128)} %get-tuple-element.28.part), custom_call_target="tpu_custom_call" | custom-call | tf_op jit(solution)/shard_map/device_sum/pallas_call | solution.py:442
  101.0 1.9 %copy.10 = f32[3,3,128,128]{3,2,1,0:T(8,128)} copy(f32[3,3,128,128]{3,2,1,0:T(8,128)} %bitcast.3) | data formatting | bytes 1179648
  102.9 1.9 %copy.11 = f32[3,3,128,128]{3,2,1,0:T(8,128)} copy(f32[3,3,128,128]{3,2,1,0:T(8,128)} %bitcast.2) | data formatting | bytes 1179648

commit v2 on v0

v2 whole, which is shorter than its diff:
```python
import functools

import jax
import jax.numpy as jnp
from jax import lax
from jax.experimental import pallas as pl
from jax.experimental.pallas import tpu as pltpu
from jax.sharding import PartitionSpec as P

MESH = pl.DeviceIdType.MESH
F32 = jnp.float32
BF16 = jnp.bfloat16
IMGS = 2
ROWS = 48
COLS = 192
CH = 128
HALF = COLS // 2
G_ROWS = ROWS + 4
A_ROWS = ROWS + 2
TANH_SCALE = 0.7978845608028654
CUBE_COEF = 0.044715
STEP = 8
TILE = 32
BY_ROWS = (((0,), (0,)), ((), ()))
CHUNKS = IMGS * ROWS // STEP
PER = ROWS // STEP
CHAINS = ((0, 1024), (1024, 768), (1792, 512))
CHAIN_SEMS = 14
TAP_ROWS = 3 * CH
LO, HI = pl.ds(0, CH), pl.ds(CH, CH)
WIN = 4 * CH


def gelu_both(a_val):
    sq = a_val * a_val
    tanh_val = jnp.tanh(a_val * (TANH_SCALE + (TANH_SCALE * CUBE_COEF) * sq))
    half_plus = 0.5 + 0.5 * tanh_val
    inner = (0.5 * TANH_SCALE) + (1.5 * TANH_SCALE * CUBE_COEF) * sq
    return a_val * half_plus, half_plus + ((1.0 - tanh_val * tanh_val) * a_val) * inner


def matmul_halves(lhs, rhs, out):
    count = lhs.shape[0] // 2
    for k in range(2):
        out[pl.ds(k * count, count), :] = jnp.dot(lhs[k * count:(k + 1) * count], rhs, preferred_element_type=F32)


def make_chain(base, size, first_sem, data, full, bufs, send_sem, recv_sem, place, last=6):
    core, quadrant, z, core_peer, xy_peers, z_peers = place
    half, eighth, quarter = size // 2, size // 8, size // 32
    mine0 = base + core * half
    away0 = base + half - core * half
    mine1 = mine0 + quadrant * eighth
    away1 = [mine0 + (3 - quadrant) * eighth, mine0 + (quadrant + 1 - 2 * (quadrant % 2)) * eighth,
             mine0 + (quadrant + 2 - 4 * (quadrant // 2)) * eighth]
    mine2 = mine1 + z * quarter
    away2 = [mine1 + ((z + 1 + t) % 4) * quarter for t in range(3)]
    slots1 = [half + t * eighth for t in range(3)]
    slots2 = [half + 3 * eighth + t * quarter for t in range(3)]

    def rows(ref, start, count):
        return ref.at[pl.ds(pl.multiple_of(start, 8), count)]

    def remote(src, dst, sem, peer):
        return pltpu.make_async_remote_copy(src_ref=src, dst_ref=dst, send_sem=send_sem.at[first_sem + sem],
                                            recv_sem=recv_sem.at[first_sem + sem], device_id=peer, device_id_type=MESH)

    def same(start, count, sem, peer):
        return remote(rows(full, start, count), rows(full, start, count), sem, peer)

    stages = [
        lambda: [remote(rows(data, away0, half), rows(bufs, 0, half), 0, core_peer)],
        lambda: [remote(rows(data, away1[t], eighth), rows(bufs, slots1[t], eighth), 1 + t, xy_peers[t]) for t in range(3)],
        lambda: [remote(rows(data, away2[t], quarter), rows(bufs, slots2[t], quarter), 4 + t, z_peers[t]) for t in range(3)],
        lambda: [same(mine2, quarter, 7 + t, z_peers[t]) for t in range(3)],
        lambda: [same(mine1, eighth, 10 + t, xy_peers[t]) for t in range(3)],
        lambda: [same(mine0, half, 13, core_peer)],
    ]
    adds = [(data, mine0, half, [0]), (data, mine1, eighth, slots1), (full, mine2, quarter, slots2)]

    def step(k):
        if k > 0:
            for copy in stages[k - 1]():
                copy.wait_recv()
        if 0 < k <= len(adds):
            dst, start, count, slots = adds[k - 1]
            spot = pl.ds(pl.multiple_of(start, 8), count)
            total = data[spot, :]
            for slot in slots:
                total = total + bufs[pl.ds(slot, count), :]
            dst[spot, :] = total
        if k < last:
            for copy in stages[k]():
                copy.start()
        else:
            for stage in stages[:last]:
                for copy in stage():
                    copy.wait_send()

    return step


def block_kernel(n_row, n_col, x_hbm, a_hbm, g_hbm, w1, w2, dx_hbm, out,
                 g_buf, a_buf, x_buf, g4, d4, band1, band2, w9, acc1, acc2, dz0, dz1, zb0, zb1, xp,
                 s_g, s_a, s_e, s_o, gcol, acol, dcol,
                 strip, pack_l, pack_r, rl, rr, corners, data, full, bufs0, bufs1, bufs2,
                 in_sem, out_sem, loc_sem, hsend_sem, hrecv_sem, send_sem, recv_sem):
    row, col = lax.axis_index("row"), lax.axis_index("col")
    x, core, z, y = row // 2, row % 2, col // 2, col % 2
    x_peer, y_peer = (col, 2 * (1 - x) + core), (2 * z + 1 - y, row)
    core_peer = (col, 2 * x + 1 - core)
    z_peers = [(2 * ((z + t) % 4) + y, row) for t in (1, 2, 3)]
    xy_peers = [(y_peer[0], x_peer[1]), y_peer, x_peer]
    place = (core, 2 * x + y, z, core_peer, xy_peers, z_peers)
    chain0, chain1, chain2 = (make_chain(*rows, CHAIN_SEMS * k, data, full, bufs, send_sem, recv_sem, place)
                              for k, (rows, bufs) in enumerate(zip(CHAINS, (bufs0, bufs1, bufs2))))

    has_n, has_s, has_w, has_e = row > 0, row < n_row - 1, col > 0, col < n_col - 1
    dirs = {
        "n": (has_n, row - 1, col), "s": (has_s, row + 1, col),
        "w": (has_w, row, col - 1), "e": (has_e, row, col + 1),
        "nw": (has_n & has_w, row - 1, col - 1), "ne": (has_n & has_e, row - 1, col + 1),
        "sw": (has_s & has_w, row + 1, col - 1), "se": (has_s & has_e, row + 1, col + 1),
    }
    barrier = pltpu.get_barrier_semaphore()
    for ok, r, c in dirs.values():
        @pl.when(ok)
        def _(r=r, c=c):
            pl.semaphore_signal(barrier, inc=1, device_id=(c, r), device_id_type=MESH)
    for peer in (core_peer, *xy_peers, *z_peers):
        pl.semaphore_signal(barrier, inc=1, device_id=peer, device_id_type=MESH)
    strips = [pltpu.make_async_copy(src.at[:, :, pl.ds(c0, 16), :], strip.at[k], loc_sem.at[k])
              for k, (src, c0) in enumerate(((g_hbm, 0), (g_hbm, COLS - 16), (a_hbm, 0), (a_hbm, COLS - 16)))]
    for cp in strips:
        cp.start()
    loads = [[pltpu.make_async_copy(src.at[m], dst, in_sem.at[m, j]) for j, (src, dst) in enumerate((
        (g_hbm, g_buf.at[m, pl.ds(2, ROWS)]), (a_hbm, a_buf.at[m, pl.ds(1, ROWS)]), (x_hbm, x_buf.at[m])))] for m in range(IMGS)]
    for j in range(3):
        for m in range(IMGS):
            loads[m][j].start()
    for ok, views in ((has_n, [g_buf.at[:, pl.ds(0, 2)], a_buf.at[:, pl.ds(0, 1)]]),
                      (has_s, [g_buf.at[:, pl.ds(ROWS + 2, 2)], a_buf.at[:, pl.ds(ROWS + 1, 1)]]),
                      (has_w, [rl]), (has_e, [rr]),
                      (dirs["nw"][0], [corners.at[0]]), (dirs["ne"][0], [corners.at[1]]),
                      (dirs["sw"][0], [corners.at[2]]), (dirs["se"][0], [corners.at[3]])):
        @pl.when(jnp.logical_not(ok))
        def _(views=views):
            for view in views:
                view[...] = jnp.zeros(view.shape, BF16)
    n_s, w_e = has_n.astype(jnp.int32) + has_s.astype(jnp.int32), has_w.astype(jnp.int32) + has_e.astype(jnp.int32)
    pl.semaphore_wait(barrier, n_s + w_e + n_s * w_e + 7)

    copies = [
        ("s", "n", g_hbm.at[:, pl.ds(ROWS - 2, 2)], g_buf.at[:, pl.ds(0, 2)]),
        ("n", "s", g_hbm.at[:, pl.ds(0, 2)], g_buf.at[:, pl.ds(ROWS + 2, 2)]),
        ("s", "n", a_hbm.at[:, pl.ds(ROWS - 1, 1)], a_buf.at[:, pl.ds(0, 1)]),
        ("n", "s", a_hbm.at[:, pl.ds(0, 1)], a_buf.at[:, pl.ds(ROWS + 1, 1)]),
        ("e", "w", pack_r, rl),
        ("w", "e", pack_l, rr),
        ("se", "nw", pack_r.at[:, :, pl.ds(32, 16)], corners.at[0]),
        ("sw", "ne", pack_l.at[:, :, pl.ds(32, 16)], corners.at[1]),
        ("ne", "sw", pack_r.at[:, :, pl.ds(0, 16)], corners.at[2]),
        ("nw", "se", pack_l.at[:, :, pl.ds(0, 16)], corners.at[3]),
    ]

    def rcopy(k, where):
        _, r, c = dirs[where]
        return pltpu.make_async_remote_copy(src_ref=copies[k][2], dst_ref=copies[k][3], send_sem=hsend_sem.at[k],
                                            recv_sem=hrecv_sem.at[k], device_id=(c, r), device_id_type=MESH)

    def start_halo(k):
        @pl.when(dirs[copies[k][0]][0])
        def _():
            rcopy(k, copies[k][0]).start()

    for k in range(4):
        start_halo(k)
    for k in range(4):
        strips[k].wait()
        pack = pack_l if k % 2 == 0 else pack_r
        for m in range(IMGS):
            s_g[pl.ds(0, ROWS * 16), :] = strip[k, m].astype(F32).reshape(ROWS * 16, CH)
            for slot, first_col in (((0, 0 if k == 0 else 14), (1, 1 if k == 0 else 15)) if k < 2 else ((2, 0 if k == 2 else 15),)):
                pack[m, slot] = s_g[pl.ds(first_col, ROWS, stride=16), :].astype(BF16)
    for k in range(4, 10):
        start_halo(k)

    for w, band in ((w1, band1), (w2, band2)):
        for dri in range(3):
            band[pl.ds(dri * 512 + 384, CH), LO] = jnp.zeros((CH, CH), BF16)
            band[pl.ds(dri * 512, CH), HI] = jnp.zeros((CH, CH), BF16)
        for a in range(3):
            for c in range(3):
                tap = w[a, c].astype(F32).T.astype(BF16)
                dri = 2 - a
                band[pl.ds(dri * 512 + (2 - c) * CH, CH), LO] = tap
                band[pl.ds(dri * 512 + (3 - c) * CH, CH), HI] = tap
                if w is w2:
                    w9[pl.ds((dri * 3 + 2 - c) * CH, CH), :] = tap
    acc1[...] = jnp.zeros_like(acc1)
    acc2[...] = jnp.zeros_like(acc2)
    zb1[...] = jnp.zeros_like(zb1)

    def window_row(m, r, t):
        base = t * 208
        s_g[pl.ds(base + 8, COLS), :] = g_buf[m, r].astype(F32)
        at = pl.multiple_of((m * G_ROWS + r) * HALF, TILE)
        for q in range(4):
            g4[pl.ds(at, HALF), pl.ds(q * CH, CH)] = s_g[pl.ds(base + 7 + q, HALF, stride=2), :].astype(BF16)

    def build_g4(n, carry):
        for t in range(4):
            window_row(n // 12, 2 + (n % 12) * 4 + t, t)
        return carry

    def prep_x(n, carry):
        m, r0 = n // PER, (n % PER) * STEP
        at = pl.multiple_of(n * STEP * HALF, TILE)
        for t in range(STEP):
            s_a[pl.ds(t * COLS, COLS), :] = x_buf[m, r0 + t].astype(F32)
            for q in range(2):
                xp[pl.ds(at + t * HALF, HALF), pl.ds(q * CH, CH)] = s_a[pl.ds(t * COLS + q, HALF, stride=2), :].astype(BF16)
        return carry

    s_g[...] = jnp.zeros_like(s_g)
    for m in range(IMGS):
        loads[m][0].wait()
    lax.fori_loop(0, 24, build_g4, 0)
    for m in range(IMGS):
        loads[m][2].wait()
    lax.fori_loop(0, CHUNKS, prep_x, 0)

    for k in range(10):
        to, frm = copies[k][:2]
        @pl.when(dirs[to][0])
        def _():
            rcopy(k, to).wait_send()
        @pl.when(dirs[frm][0])
        def _():
            rcopy(k, frm).wait_recv()

    for side, (beside, top, bot) in enumerate(((rl, 0, 2), (rr, 1, 3))):
        for m in range(IMGS):
            for k in range(2):
                slot = k if side == 0 else k + 1
                gcol[side, m, slot, pl.ds(8, ROWS), :] = beside[m, k].astype(F32)
                gcol[side, m, slot, pl.ds(6, 2), :] = corners[top, m, k].astype(F32)[14:16]
                gcol[side, m, slot, pl.ds(8 + ROWS, 2), :] = corners[bot, m, k].astype(F32)[0:2]
            acol[side, m, pl.ds(8, ROWS), :] = beside[m, 2].astype(F32)
            acol[side, m, pl.ds(7, 1), :] = corners[top, m, 2].astype(F32)[15:16]
            acol[side, m, pl.ds(8 + ROWS, 1), :] = corners[bot, m, 2].astype(F32)[0:1]
    for m in range(IMGS):
        for side in range(2):
            edge = g_buf[m, :, pl.ds(0 if side == 0 else COLS - 16, 16), :].astype(F32)
            s_g[pl.ds(0, G_ROWS * 16), :] = edge.reshape(G_ROWS * 16, CH)
            gcol[side, m, 2 if side == 0 else 0, pl.ds(6, G_ROWS), :] = s_g[pl.ds(0 if side == 0 else 15, G_ROWS, stride=16), :]
    lhs = jnp.concatenate([jnp.concatenate(
        [gcol[side, m, dci, pl.ds(6 + dri, 64), :].astype(BF16) for dri in range(3) for dci in range(3)], axis=1)
        for side in range(2) for m in range(IMGS)], axis=0)
    dz_col = jnp.dot(lhs, w9[...], preferred_element_type=F32)
    for side, inside in ((0, has_w), (1, has_e)):
        for m in range(IMGS):
            _, slope = gelu_both(acol[side, m, pl.ds(7, 64), :])
            first_row = (side * IMGS + m) * 64
            dcol[side, m] = jnp.where(inside, dz_col[first_row:first_row + 64] * slope, 0.0)

    for m in range(IMGS):
        for t, r in enumerate((0, 1, G_ROWS - 2, G_ROWS - 1)):
            window_row(m, r, t)
    line = lax.broadcasted_iota(jnp.int32, (16, CH), 0)

    def patch(n, carry):
        for t in range(4):
            for m in range(IMGS):
                r = n * 4 + t
                at = pl.multiple_of((m * G_ROWS + r) * HALF, TILE)
                for side, where, q, hit in ((0, at, 0, 0), (1, at + HALF - 16, 3, 15)):
                    spot = (pl.ds(pl.multiple_of(where, 16), 16), pl.ds(q * CH, CH))
                    new = jnp.broadcast_to(gcol[side, m, 1, pl.ds(6 + r, 1), :], (16, CH))
                    g4[spot] = jnp.where(line == hit, new, g4[spot].astype(F32)).astype(BF16)
        return carry

    lax.fori_loop(0, 13, patch, 0)
    for m in range(IMGS):
        loads[m][1].wait()

    def g_rows(m, r, count):
        return g4[pl.ds(pl.multiple_of((m * G_ROWS + r) * HALF, TILE), count * HALF), :]

    def d_rows(m, r, count):
        return d4[pl.ds(pl.multiple_of((m * A_ROWS + r) * HALF, TILE), count * HALF), :]

    def one_row(m, d, t, dz, zb):
        base = t * COLS
        s_a[pl.ds(base, COLS), :] = a_buf[m, d].astype(F32)
        at = pl.multiple_of((m * A_ROWS + d) * HALF, TILE)
        z_e, slope_e = gelu_both(s_a[pl.ds(base, HALF, stride=2), :])
        z_o, slope_o = gelu_both(s_a[pl.ds(base + 1, HALF, stride=2), :])
        if zb is not None:
            zb[pl.ds(t * HALF, HALF), LO] = z_e.astype(BF16)
            zb[pl.ds(t * HALF, HALF), HI] = z_o.astype(BF16)
        da_e = dz[pl.ds(t * HALF, HALF), LO] * slope_e
        da_o = dz[pl.ds(t * HALF, HALF), HI] * slope_o
        s_e[t, pl.ds(8, HALF), :] = da_e
        s_o[t, pl.ds(8, HALF), :] = da_o
        s_o[t, pl.ds(7, 1), :] = dcol[0, m, pl.ds(d, 1), :]
        s_e[t, pl.ds(8 + HALF, 1), :] = dcol[1, m, pl.ds(d, 1), :]
        d4[pl.ds(at, HALF), LO] = s_o[t, pl.ds(7, HALF), :].astype(BF16)
        d4[pl.ds(at, HALF), HI] = da_e.astype(BF16)
        d4[pl.ds(at, HALF), pl.ds(2 * CH, CH)] = da_o.astype(BF16)
        d4[pl.ds(at, HALF), pl.ds(3 * CH, CH)] = s_e[t, pl.ds(9, HALF), :].astype(BF16)

    frame = [(m, d) for m in range(IMGS) for d in (0, A_ROWS - 1)]
    lhs = jnp.concatenate([jnp.concatenate([g_rows(m, d + t, 1) for t in range(3)], axis=1) for m, d in frame], axis=0)
    matmul_halves(lhs, band2[...], dz0)
    for t, (m, d) in enumerate(frame):
        one_row(m, d, t, dz0, None)
    for edge, ok in ((0, has_n), (A_ROWS - 1, has_s)):
        @pl.when(jnp.logical_not(ok))
        def _(edge=edge):
            for m in range(IMGS):
                d4[pl.ds((m * A_ROWS + edge) * HALF, HALF), :] = jnp.zeros((HALF, 4 * CH), BF16)

    def conv_a(n, out):
        m, r0 = n // PER, (n % PER) * STEP
        lhs = jnp.concatenate([g_rows(m, r0 + 1 + t, STEP) for t in range(3)], axis=1)
        matmul_halves(lhs, band2[...], out)

    def grad2(n, zb):
        m, r0 = n // PER, (n % PER) * STEP
        win = jnp.concatenate([g_rows(m, r0 + 1 + t, STEP) for t in range(3)], axis=1)
        acc2[...] += lax.dot_general(zb[...], win, BY_ROWS, preferred_element_type=F32)

    conv_a(0, dz0)

    def step_a(i, carry):
        for n, dz, dz_next, zb, zb_last in ((2 * i, dz0, dz1, zb0, zb1), (2 * i + 1, dz1, dz0, zb1, zb0)):
            m, r0 = n // PER, (n % PER) * STEP
            conv_a(jnp.minimum(n + 1, CHUNKS - 1), dz_next)
            grad2(jnp.maximum(n - 1, 0), zb_last)
            for t in range(STEP):
                one_row(m, r0 + 1 + t, t, dz, zb)
        return carry

    lax.fori_loop(0, CHUNKS // 2, step_a, 0)
    grad2(CHUNKS - 1, zb1)

    def fold(acc, a, at):
        for c in range(3):
            left, top = (2 - a) * WIN + (2 - c) * CH, at + c * CH
            data[pl.ds(top, CH), :] = acc[LO, pl.ds(left, CH)] + acc[HI, pl.ds(left + CH, CH)]

    for a in range(3):
        fold(acc2, a, a * TAP_ROWS)
    chain0(0)

    def at_steps(i, table):
        for when, chain, k in table:
            def run(_, carry, chain=chain, k=k):
                chain(k)
                return carry

            lax.fori_loop(0, (i == when).astype(jnp.int32), run, 0)

    def grad1(i, dris):
        m, r0 = i // 3, (i % 3) * 2 * STEP
        win = jnp.concatenate([d_rows(m, r0 + t, 2 * STEP) for t in dris], axis=1)
        x_rows = xp[pl.ds(pl.multiple_of(i * 2 * STEP * HALF, TILE), 2 * STEP * HALF), :]
        spot = pl.ds(dris[0] * WIN, len(dris) * WIN)
        acc1[:, spot] += lax.dot_general(x_rows, win, BY_ROWS, preferred_element_type=F32)

    def step_b(i, carry):
        at_steps(i, ((2, chain0, 1),))
        grad1(i, (0, 1))
        return carry

    def step_b2(i, carry):
        at_steps(i, ((1, chain0, 2), (3, chain1, 1)))
        grad1(i, (2,))
        return carry

    lax.fori_loop(0, CHUNKS // 2, step_b, 0)
    fold(acc1, 1, 3 * TAP_ROWS)
    fold(acc1, 2, 4 * TAP_ROWS)
    chain1(0)
    lax.fori_loop(0, CHUNKS // 2, step_b2, 0)
    fold(acc1, 0, 5 * TAP_ROWS)
    chain2(0)

    def conv_x(n, out):
        m, r0 = n // PER, (n % PER) * STEP
        win = jnp.concatenate([d_rows(m, r0 + t, STEP) for t in range(3)], axis=1)
        matmul_halves(win, band1[...], out)

    def out_copy(n):
        rows = pl.ds((n % PER) * STEP, STEP)
        return pltpu.make_async_copy(x_buf.at[n // PER, rows], dx_hbm.at[n // PER, rows], out_sem.at[n])

    def finish(n, dz):
        m, r0 = n // PER, (n % PER) * STEP
        own = g4[pl.ds(pl.multiple_of((m * G_ROWS + r0 + 2) * HALF, TILE), STEP * HALF), pl.ds(CH, 2 * CH)].astype(F32)
        for t in range(STEP):
            part = dz[pl.ds(t * HALF, HALF), :] + own[t * HALF:(t + 1) * HALF]
            for q in range(2):
                s_a[pl.ds(t * COLS + q, HALF, stride=2), :] = part[:, q * CH:(q + 1) * CH]
            x_buf[m, r0 + t] = s_a[pl.ds(t * COLS, COLS), :].astype(BF16)
        out_copy(n).start()

    conv_x(0, dz0)

    def step_c(i, carry):
        at_steps(i, ((1, chain2, 1), (3, chain2, 2), (5, chain2, 3)))
        conv_x(2 * i + 1, dz1)
        finish(2 * i, dz0)
        at_steps(i, ((0, chain0, 3), (1, chain1, 2), (2, chain0, 4), (3, chain1, 3), (4, chain0, 5), (5, chain1, 4)))
        conv_x(jnp.minimum(2 * i + 2, CHUNKS - 1), dz0)
        finish(2 * i + 1, dz1)
        return carry

    lax.fori_loop(0, CHUNKS // 2, step_c, 0)
    for chain, k in ((chain0, 6), (chain1, 5), (chain2, 4), (chain1, 6), (chain2, 5), (chain2, 6)):
        chain(k)
    result = pltpu.make_async_copy(full, out, loc_sem.at[0])
    result.start()
    for n in range(CHUNKS):
        out_copy(n).wait()
    result.wait()


def place_kernel(dx_in, dw_in, dx_out, dw1_out, dw2_out, dx_buf, dw_buf, in_sem, out_sem):
    halves = ROWS // 2
    pieces = [(dx_in.at[k // 2, pl.ds(k % 2 * halves, halves)], dx_buf.at[k // 2, pl.ds(k % 2 * halves, halves)],
               dx_out.at[k // 2, pl.ds(k % 2 * halves, halves)]) for k in range(4)]
    for k, (dst, at) in enumerate(((dw2_out, 0), (dw1_out, 5), (dw1_out, 3))):
        count = (3, 1, 2)[k] * TAP_ROWS
        rows = pl.ds(at * TAP_ROWS, count)
        pieces.append((dw_in.at[rows], dw_buf.at[rows], dst.at[pl.ds((0, 0, TAP_ROWS)[k], count)]))
    loads = [pltpu.make_async_copy(src, mid, in_sem.at[k]) for k, (src, mid, _) in enumerate(pieces)]
    stores = [pltpu.make_async_copy(mid, dst, out_sem.at[k]) for k, (_, mid, dst) in enumerate(pieces)]
    for copy in loads:
        copy.start()
    for load, store in zip(loads, stores):
        load.wait()
        store.start()
    for store in stores:
        store.wait()


def place_results(d_x, dw):
    hbm = pl.BlockSpec(memory_space=pl.ANY)
    taps = jax.ShapeDtypeStruct((9 * CH, CH), F32)
    return pl.pallas_call(
        place_kernel,
        out_shape=[jax.ShapeDtypeStruct(d_x.shape, BF16), taps, taps],
        in_specs=[hbm] * 2,
        out_specs=[hbm] * 3,
        scratch_shapes=[pltpu.VMEM(d_x.shape, BF16), pltpu.VMEM(dw.shape, F32), pltpu.SemaphoreType.DMA((7,)), pltpu.SemaphoreType.DMA((7,))],
        name="place_results",
    )(d_x, dw)


def block_grads(mesh_shape, x_tile, a_tile, g_tile, w_one, w_two):
    vm = pl.BlockSpec(memory_space=pltpu.VMEM)
    hbm = pl.BlockSpec(memory_space=pl.ANY)
    half, pair = STEP * HALF, 2 * CH
    padded, cols = (STEP, HALF + 16, CH), (IMGS, 3, ROWS, CH)
    return pl.pallas_call(
        functools.partial(block_kernel, mesh_shape["row"], mesh_shape["col"]),
        out_shape=[jax.ShapeDtypeStruct((IMGS, ROWS, COLS, CH), BF16), jax.ShapeDtypeStruct((18 * CH, CH), F32)],
        in_specs=[hbm] * 3 + [vm] * 2,
        out_specs=[hbm] * 2,
        scratch_shapes=[pltpu.VMEM(shape, BF16) for shape in (
            (IMGS, G_ROWS, COLS, CH), (IMGS, A_ROWS, COLS, CH), (IMGS, ROWS, COLS, CH),
            (IMGS * G_ROWS * HALF, WIN), (IMGS * A_ROWS * HALF, WIN), (3 * WIN, pair), (3 * WIN, pair), (9 * CH, CH))
        ] + [pltpu.VMEM(shape, F32) for shape in ((pair, 3 * WIN), (pair, 3 * WIN), (half, pair), (half, pair))
        ] + [pltpu.VMEM(shape, BF16) for shape in ((half, pair), (half, pair), (CHUNKS * half, pair))
        ] + [pltpu.VMEM(shape, F32) for shape in (
            (4 * 208 + 16, CH), (STEP * COLS, CH), padded, padded, (2, IMGS, 3, 72, CH), (2, IMGS, 72, CH), (2, IMGS, 64, CH))
        ] + [pltpu.VMEM(shape, BF16) for shape in ((4, IMGS, ROWS, 16, CH), cols, cols, cols, cols, (4, IMGS, 3, 16, CH))
        ] + [pltpu.VMEM(shape, F32) for shape in ((18 * CH, CH), (18 * CH, CH), *((size, CH) for _, size in CHAINS))
        ] + [pltpu.SemaphoreType.DMA(shape) for shape in ((IMGS, 3), (CHUNKS,), (4,), (10,), (10,), (3 * CHAIN_SEMS,), (3 * CHAIN_SEMS,))],
        compiler_params=pltpu.CompilerParams(collective_id=0, has_side_effects=True, vmem_limit_bytes=67043328),
        name="block_grads",
    )(x_tile, a_tile, g_tile, w_one, w_two)


def solution(mesh):
    shape = dict(mesh.shape)

    def local_step(x_tile, a_tile, g_tile, w_one, w_two):
        d_x, dw = block_grads(shape, x_tile, a_tile, g_tile, w_one, w_two)
        d_x, d_w1, d_w2 = place_results(d_x, dw)
        return d_x, d_w1.reshape(w_one.shape), d_w2.reshape(w_two.shape)

    tile_spec = P(None, "row", "col", None)
    return jax.shard_map(local_step, mesh=mesh, in_specs=(tile_spec, tile_spec, tile_spec, P(), P()), out_specs=(tile_spec, P(), P()), check_vma=False)
```

time: 368 us -> 77.5 us (0.21); the launches traced: 363 us -> 77.4 us
  waiting for transfers between devices: 123 us -> 0 us
  matrix products: 86.9 us -> 0 us
  Pallas kernels: 0 us -> 76.8 us
  local copies, waits for them, and re-layouts: 64.2 us -> 0 us
  other arithmetic: 50.6 us -> 0 us
  starting transfers between devices: 22.9 us -> 0 us
  between operations: 14.8 us -> 0.64 us
    psum x1 -> x0, waiting for transfers between devices: 122 us -> none  [local_step(): d_w1, d_w2 = lax.psum((w1_part, w2_part), ('row', 'col'))]
    pallas_call x0 -> x2, Pallas kernels: none -> 76.8 us  [the longest x1 72 us: block_grads(): pl.pallas_call(functools.partial(block_kernel, mesh_shape['row'], mesh_sh...]
    dot_general x18 -> x0, matrix products: 60.5 us -> none  [tap_grads(): jnp.einsum('bhwi,bhwo->io', tile_in, grad_wide[:, 2 - tap_row:2 - tap_row...]
    conv_general_dilated x2 -> x0, matrix products: 26.4 us -> none  [conv_valid(): lax.conv_general_dilated(lhs_arr, rhs_arr, (1, 1), 'VALID', dimension_num...]
    unnamed x37 -> x0, local copies, waits for them, and re-layouts: 25.5 us -> none
    ppermute x8 -> x0, starting transfers between devices: 22.8 us -> none  [the longest x2 9.38 us: add_halo(): from_left = lax.ppermute(tall[:, :, -1:], 'col', col_down)]
    conv_general_dilated x5 -> x0, local copies, waits for them, and re-layouts: 20.5 us -> none  [conv_valid(): lax.conv_general_dilated(lhs_arr, rhs_arr, (1, 1), 'VALID', dimension_num...]
    convert_element_type x2 -> x0, other arithmetic: 17.8 us -> none  [the longest x1 9.6 us: local_step(): d_a = (d_z * gelu_slope(a_val)).astype(jnp.bfloat16)]
  transfers between devices with their start and end apart: 9 -> 0, of which waited for: 2 -> 0; matrix products, arithmetic and copies ran while one was open for 18% -> 0% of each run, Pallas kernels for 0% -> 0%
where the time goes in v2:
time: 77.5 us; the launch traced here: 77.4 us
  Pallas kernels  76.8 us (99%)
    pallas_call x1, Pallas kernels, block_grads(): pl.pallas_call(functools.partial(block_kernel, mesh_shape['row'], mesh_sh...  72 us
    pallas_call x1, Pallas kernels, place_results(): pl.pallas_call(place_kernel, out_shape=[jax.ShapeDtypeStruct(d_x.shape, B...  4.73 us

profile of v2, /device:TPU:0, one launch (start us, length us, event | category | flops | bytes accessed | tf_op | source)
XLA Modules:
  0.0 77.4 jit_solution(13316702868715929056)
XLA Ops:
  0.6 72.0 %block_grads.1 = (bf16[2,48,192,128]{3,2,1,0:T(8,128)(2,1)}, f32[2304,128]{1,0:T(8,128)}) custom-call(bf16[2,48,192,128]{3,2,1,0:T(8,128)(2,1)} %x_hbm.1, bf16[2,48,192,128]{3,2,1,0:T(8,128)(2,1)} %a_hbm.1, bf16[2,48,192,128]{3,2,1,0:T(8,128)(2,1)} %g_hbm.1, bf16[3,3,128,128]{3,2,1,0:T(8,128)(2,1)} %w1.1, bf16[3,3,128,128]{3,2,1,0:T(8,128)(2,1)} %w2.1), custom_call_target="tpu_custom_call" | custom-call | tf_op jit(solution)/shard_map/block_grads/pallas_call | solution.py:467
  72.7 4.7 %place_results.1 = (bf16[2,48,192,128]{3,2,1,0:T(8,128)(2,1)}, f32[1152,128]{1,0:T(8,128)}, f32[1152,128]{1,0:T(8,128)}) custom-call(bf16[2,48,192,128]{3,2,1,0:T(8,128)(2,1)} %get-tuple-element.8.dx_in, f32[2304,128]{1,0:T(8,128)} %get-tuple-element.9.dw_in), custom_call_target="tpu_custom_call" | custom-call | tf_op jit(solution)/shard_map/place_results/pallas_call | solution.py:452

commit v3 on v2

--- a/solution.py
+++ b/solution.py
@@ -25,7 +25,13 @@
 CHUNKS = IMGS * ROWS // STEP
 PER = ROWS // STEP
 CHAINS = ((0, 1024), (1024, 768), (1792, 512))
+A_STEP = 6
+A_PER = ROWS // A_STEP
+A_UNROLL = 2
+TURNS = 1
 CHAIN_SEMS = 14
+BLOCK_BYTES = 61145088
+PLACE_BYTES = 1048576
 TAP_ROWS = 3 * CH
 LO, HI = pl.ds(0, CH), pl.ds(CH, CH)
 WIN = 4 * CH
@@ -100,11 +106,11 @@
     return step
 
 
-def block_kernel(n_row, n_col, x_hbm, a_hbm, g_hbm, w1, w2, dx_hbm, out,
-                 g_buf, a_buf, x_buf, g4, d4, band1, band2, w9, acc1, acc2, dz0, dz1, zb0, zb1, xp,
+def block_kernel(n_row, n_col, x_hbm, a_hbm, g_hbm, w1, w2, x_buf, full,
+                 g_buf, a_buf, g4, d4, band1, band2, w9, acc1, acc2, dz0, dz1, zp, xp,
                  s_g, s_a, s_e, s_o, gcol, acol, dcol,
-                 strip, pack_l, pack_r, rl, rr, corners, data, full, bufs0, bufs1, bufs2,
-                 in_sem, out_sem, loc_sem, hsend_sem, hrecv_sem, send_sem, recv_sem):
+                 strip, pack_l, pack_r, rl, rr, corners, data, bufs0, bufs1, bufs2,
+                 in_sem, loc_sem, hsend_sem, hrecv_sem, send_sem, recv_sem):
     row, col = lax.axis_index("row"), lax.axis_index("col")
     x, core, z, y = row // 2, row % 2, col // 2, col % 2
     x_peer, y_peer = (col, 2 * (1 - x) + core), (2 * z + 1 - y, row)
@@ -199,7 +205,6 @@
                     w9[pl.ds((dri * 3 + 2 - c) * CH, CH), :] = tap
     acc1[...] = jnp.zeros_like(acc1)
     acc2[...] = jnp.zeros_like(acc2)
-    zb1[...] = jnp.zeros_like(zb1)
 
     def window_row(m, r, t):
         base = t * 208
@@ -290,31 +295,33 @@
     def d_rows(m, r, count):
         return d4[pl.ds(pl.multiple_of((m * A_ROWS + r) * HALF, TILE), count * HALF), :]
 
-    def one_row(m, d, t, dz, zb):
-        base = t * COLS
+    def one_row(m, d, t, dz, inside):
+        turn = t % TURNS
+        base = turn * COLS
         s_a[pl.ds(base, COLS), :] = a_buf[m, d].astype(F32)
         at = pl.multiple_of((m * A_ROWS + d) * HALF, TILE)
         z_e, slope_e = gelu_both(s_a[pl.ds(base, HALF, stride=2), :])
         z_o, slope_o = gelu_both(s_a[pl.ds(base + 1, HALF, stride=2), :])
-        if zb is not None:
-            zb[pl.ds(t * HALF, HALF), LO] = z_e.astype(BF16)
-            zb[pl.ds(t * HALF, HALF), HI] = z_o.astype(BF16)
+        if inside:
+            z_at = pl.multiple_of((m * ROWS + d - 1) * HALF, TILE)
+            zp[pl.ds(z_at, HALF), LO] = z_e.astype(BF16)
+            zp[pl.ds(z_at, HALF), HI] = z_o.astype(BF16)
         da_e = dz[pl.ds(t * HALF, HALF), LO] * slope_e
         da_o = dz[pl.ds(t * HALF, HALF), HI] * slope_o
-        s_e[t, pl.ds(8, HALF), :] = da_e
-        s_o[t, pl.ds(8, HALF), :] = da_o
-        s_o[t, pl.ds(7, 1), :] = dcol[0, m, pl.ds(d, 1), :]
-        s_e[t, pl.ds(8 + HALF, 1), :] = dcol[1, m, pl.ds(d, 1), :]
-        d4[pl.ds(at, HALF), LO] = s_o[t, pl.ds(7, HALF), :].astype(BF16)
+        s_e[turn, pl.ds(8, HALF), :] = da_e
+        s_o[turn, pl.ds(8, HALF), :] = da_o
+        s_o[turn, pl.ds(7, 1), :] = dcol[0, m, pl.ds(d, 1), :]
+        s_e[turn, pl.ds(8 + HALF, 1), :] = dcol[1, m, pl.ds(d, 1), :]
+        d4[pl.ds(at, HALF), LO] = s_o[turn, pl.ds(7, HALF), :].astype(BF16)
         d4[pl.ds(at, HALF), HI] = da_e.astype(BF16)
         d4[pl.ds(at, HALF), pl.ds(2 * CH, CH)] = da_o.astype(BF16)
-        d4[pl.ds(at, HALF), pl.ds(3 * CH, CH)] = s_e[t, pl.ds(9, HALF), :].astype(BF16)
+        d4[pl.ds(at, HALF), pl.ds(3 * CH, CH)] = s_e[turn, pl.ds(9, HALF), :].astype(BF16)
 
     frame = [(m, d) for m in range(IMGS) for d in (0, A_ROWS - 1)]
     lhs = jnp.concatenate([jnp.concatenate([g_rows(m, d + t, 1) for t in range(3)], axis=1) for m, d in frame], axis=0)
     matmul_halves(lhs, band2[...], dz0)
     for t, (m, d) in enumerate(frame):
-        one_row(m, d, t, dz0, None)
+        one_row(m, d, t, dz0, False)
     for edge, ok in ((0, has_n), (A_ROWS - 1, has_s)):
         @pl.when(jnp.logical_not(ok))
         def _(edge=edge):
@@ -322,28 +329,37 @@
                 d4[pl.ds((m * A_ROWS + edge) * HALF, HALF), :] = jnp.zeros((HALF, 4 * CH), BF16)
 
     def conv_a(n, out):
-        m, r0 = n // PER, (n % PER) * STEP
-        lhs = jnp.concatenate([g_rows(m, r0 + 1 + t, STEP) for t in range(3)], axis=1)
+        m, r0 = n // A_PER, (n % A_PER) * A_STEP
+        lhs = jnp.concatenate([g_rows(m, r0 + 1 + t, A_STEP) for t in range(3)], axis=1)
         matmul_halves(lhs, band2[...], out)
 
-    def grad2(n, zb):
-        m, r0 = n // PER, (n % PER) * STEP
-        win = jnp.concatenate([g_rows(m, r0 + 1 + t, STEP) for t in range(3)], axis=1)
-        acc2[...] += lax.dot_general(zb[...], win, BY_ROWS, preferred_element_type=F32)
-
     conv_a(0, dz0)
 
     def step_a(i, carry):
-        for n, dz, dz_next, zb, zb_last in ((2 * i, dz0, dz1, zb0, zb1), (2 * i + 1, dz1, dz0, zb1, zb0)):
-            m, r0 = n // PER, (n % PER) * STEP
-            conv_a(jnp.minimum(n + 1, CHUNKS - 1), dz_next)
-            grad2(jnp.maximum(n - 1, 0), zb_last)
-            for t in range(STEP):
-                one_row(m, r0 + 1 + t, t, dz, zb)
-        return carry
-
-    lax.fori_loop(0, CHUNKS // 2, step_a, 0)
-    grad2(CHUNKS - 1, zb1)
+        for k in range(A_UNROLL):
+            n = A_UNROLL * i + k
+            m, r0 = n // A_PER, (n % A_PER) * A_STEP
+            dz, dz_next = ((dz0, dz1), (dz1, dz0))[k % 2] if A_UNROLL > 1 else (dz0, dz0)
+            for t in range(A_STEP):
+                one_row(m, r0 + 1 + t, t, dz, True)
+            conv_a(jnp.minimum(n + 1, IMGS * A_PER - 1), dz_next)
+        return carry
+
+    lax.fori_loop(0, IMGS * A_PER // A_UNROLL, step_a, 0)
+
+    def grad(i, pairs, windows, skip, dris, acc):
+        m, r0 = i // 3, (i % 3) * 2 * STEP
+        win = jnp.concatenate([windows(m, r0 + skip + t, 2 * STEP) for t in dris], axis=1)
+        rows = pairs[pl.ds(pl.multiple_of(i * 2 * STEP * HALF, TILE), 2 * STEP * HALF), :]
+        spot = pl.ds(dris[0] * WIN, len(dris) * WIN)
+        acc[:, spot] += lax.dot_general(rows, win, BY_ROWS, preferred_element_type=F32)
+
+    def step_z(i, carry):
+        for t in range(3):
+            grad(3 * i + t, zp, g_rows, 1, (0, 1, 2), acc2)
+        return carry
+
+    lax.fori_loop(0, IMGS, step_z, 0)
 
     def fold(acc, a, at):
         for c in range(3):
@@ -362,28 +378,23 @@
 
             lax.fori_loop(0, (i == when).astype(jnp.int32), run, 0)
 
-    def grad1(i, dris):
-        m, r0 = i // 3, (i % 3) * 2 * STEP
-        win = jnp.concatenate([d_rows(m, r0 + t, 2 * STEP) for t in dris], axis=1)
-        x_rows = xp[pl.ds(pl.multiple_of(i * 2 * STEP * HALF, TILE), 2 * STEP * HALF), :]
-        spot = pl.ds(dris[0] * WIN, len(dris) * WIN)
-        acc1[:, spot] += lax.dot_general(x_rows, win, BY_ROWS, preferred_element_type=F32)
-
     def step_b(i, carry):
-        at_steps(i, ((2, chain0, 1),))
-        grad1(i, (0, 1))
+        at_steps(i, ((1, chain0, 1),))
+        for t in range(3):
+            grad(3 * i + t, xp, d_rows, 0, (0, 1), acc1)
         return carry
 
     def step_b2(i, carry):
-        at_steps(i, ((1, chain0, 2), (3, chain1, 1)))
-        grad1(i, (2,))
-        return carry
-
-    lax.fori_loop(0, CHUNKS // 2, step_b, 0)
+        at_steps(i, ((1, chain0, 2), (1, chain1, 1)))
+        for t in range(3):
+            grad(3 * i + t, xp, d_rows, 0, (2,), acc1)
+        return carry
+
+    lax.fori_loop(0, IMGS, step_b, 0)
     fold(acc1, 1, 3 * TAP_ROWS)
     fold(acc1, 2, 4 * TAP_ROWS)
     chain1(0)
-    lax.fori_loop(0, CHUNKS // 2, step_b2, 0)
+    lax.fori_loop(0, IMGS, step_b2, 0)
     fold(acc1, 0, 5 * TAP_ROWS)
     chain2(0)
 
@@ -391,10 +402,6 @@
         m, r0 = n // PER, (n % PER) * STEP
         win = jnp.concatenate([d_rows(m, r0 + t, STEP) for t in range(3)], axis=1)
         matmul_halves(win, band1[...], out)
-
-    def out_copy(n):
-        rows = pl.ds((n % PER) * STEP, STEP)
-        return pltpu.make_async_copy(x_buf.at[n // PER, rows], dx_hbm.at[n // PER, rows], out_sem.at[n])
 
     def finish(n, dz):
         m, r0 = n // PER, (n % PER) * STEP
@@ -404,57 +411,43 @@
             for q in range(2):
                 s_a[pl.ds(t * COLS + q, HALF, stride=2), :] = part[:, q * CH:(q + 1) * CH]
             x_buf[m, r0 + t] = s_a[pl.ds(t * COLS, COLS), :].astype(BF16)
-        out_copy(n).start()
 
     conv_x(0, dz0)
 
     def step_c(i, carry):
-        at_steps(i, ((1, chain2, 1), (3, chain2, 2), (5, chain2, 3)))
+        at_steps(i, ((1, chain0, 3), (3, chain0, 4), (4, chain1, 4), (5, chain0, 5)))
         conv_x(2 * i + 1, dz1)
         finish(2 * i, dz0)
-        at_steps(i, ((0, chain0, 3), (1, chain1, 2), (2, chain0, 4), (3, chain1, 3), (4, chain0, 5), (5, chain1, 4)))
+        at_steps(i, ((0, chain2, 1), (0, chain1, 2), (2, chain2, 2), (2, chain1, 3), (4, chain2, 3)))
         conv_x(jnp.minimum(2 * i + 2, CHUNKS - 1), dz0)
         finish(2 * i + 1, dz1)
         return carry
 
     lax.fori_loop(0, CHUNKS // 2, step_c, 0)
-    for chain, k in ((chain0, 6), (chain1, 5), (chain2, 4), (chain1, 6), (chain2, 5), (chain2, 6)):
+    for chain, k in ((chain1, 5), (chain2, 4), (chain0, 6), (chain1, 6), (chain2, 5), (chain2, 6)):
         chain(k)
-    result = pltpu.make_async_copy(full, out, loc_sem.at[0])
-    result.start()
-    for n in range(CHUNKS):
-        out_copy(n).wait()
-    result.wait()
-
-
-def place_kernel(dx_in, dw_in, dx_out, dw1_out, dw2_out, dx_buf, dw_buf, in_sem, out_sem):
-    halves = ROWS // 2
-    pieces = [(dx_in.at[k // 2, pl.ds(k % 2 * halves, halves)], dx_buf.at[k // 2, pl.ds(k % 2 * halves, halves)],
-               dx_out.at[k // 2, pl.ds(k % 2 * halves, halves)]) for k in range(4)]
-    for k, (dst, at) in enumerate(((dw2_out, 0), (dw1_out, 5), (dw1_out, 3))):
-        count = (3, 1, 2)[k] * TAP_ROWS
-        rows = pl.ds(at * TAP_ROWS, count)
-        pieces.append((dw_in.at[rows], dw_buf.at[rows], dst.at[pl.ds((0, 0, TAP_ROWS)[k], count)]))
-    loads = [pltpu.make_async_copy(src, mid, in_sem.at[k]) for k, (src, mid, _) in enumerate(pieces)]
-    stores = [pltpu.make_async_copy(mid, dst, out_sem.at[k]) for k, (_, mid, dst) in enumerate(pieces)]
-    for copy in loads:
-        copy.start()
-    for load, store in zip(loads, stores):
-        load.wait()
+
+
+def place_kernel(dx_in, dw_in, dx_out, dw1_out, dw2_out, out_sem):
+    pieces = [(dx_in.at[m], dx_out.at[m]) for m in range(IMGS)]
+    for dst, at, first, count in ((dw2_out, 0, 0, 3), (dw1_out, 5, 0, 1), (dw1_out, 3, 1, 2)):
+        pieces.append((dw_in.at[pl.ds(at * TAP_ROWS, count * TAP_ROWS)], dst.at[pl.ds(first * TAP_ROWS, count * TAP_ROWS)]))
+    stores = [pltpu.make_async_copy(src, dst, out_sem.at[k]) for k, (src, dst) in enumerate(pieces)]
+    for store in stores:
         store.start()
     for store in stores:
         store.wait()
 
 
 def place_results(d_x, dw):
-    hbm = pl.BlockSpec(memory_space=pl.ANY)
     taps = jax.ShapeDtypeStruct((9 * CH, CH), F32)
     return pl.pallas_call(
         place_kernel,
-        out_shape=[jax.ShapeDtypeStruct(d_x.shape, BF16), taps, taps],
-        in_specs=[hbm] * 2,
-        out_specs=[hbm] * 3,
-        scratch_shapes=[pltpu.VMEM(d_x.shape, BF16), pltpu.VMEM(dw.shape, F32), pltpu.SemaphoreType.DMA((7,)), pltpu.SemaphoreType.DMA((7,))],
+        out_shape=[jax.ShapeDtypeStruct((IMGS, ROWS, COLS, CH), BF16), taps, taps],
+        in_specs=[pl.BlockSpec(memory_space=pltpu.VMEM)] * 2,
+        out_specs=[pl.BlockSpec(memory_space=pl.ANY)] * 3,
+        scratch_shapes=[pltpu.SemaphoreType.DMA((5,))],
+        compiler_params=pltpu.CompilerParams(vmem_limit_bytes=PLACE_BYTES),
         name="place_results",
     )(d_x, dw)
 
@@ -466,20 +459,20 @@
     padded, cols = (STEP, HALF + 16, CH), (IMGS, 3, ROWS, CH)
     return pl.pallas_call(
         functools.partial(block_kernel, mesh_shape["row"], mesh_shape["col"]),
-        out_shape=[jax.ShapeDtypeStruct((IMGS, ROWS, COLS, CH), BF16), jax.ShapeDtypeStruct((18 * CH, CH), F32)],
+        out_shape=[pltpu.VMEM((IMGS, ROWS, COLS, CH), BF16), pltpu.VMEM((18 * CH, CH), F32)],
         in_specs=[hbm] * 3 + [vm] * 2,
-        out_specs=[hbm] * 2,
+        out_specs=[vm] * 2,
         scratch_shapes=[pltpu.VMEM(shape, BF16) for shape in (
-            (IMGS, G_ROWS, COLS, CH), (IMGS, A_ROWS, COLS, CH), (IMGS, ROWS, COLS, CH),
+            (IMGS, G_ROWS, COLS, CH), (IMGS, A_ROWS, COLS, CH),
             (IMGS * G_ROWS * HALF, WIN), (IMGS * A_ROWS * HALF, WIN), (3 * WIN, pair), (3 * WIN, pair), (9 * CH, CH))
         ] + [pltpu.VMEM(shape, F32) for shape in ((pair, 3 * WIN), (pair, 3 * WIN), (half, pair), (half, pair))
-        ] + [pltpu.VMEM(shape, BF16) for shape in ((half, pair), (half, pair), (CHUNKS * half, pair))
+        ] + [pltpu.VMEM(shape, BF16) for shape in ((CHUNKS * half, pair), (CHUNKS * half, pair))
         ] + [pltpu.VMEM(shape, F32) for shape in (
             (4 * 208 + 16, CH), (STEP * COLS, CH), padded, padded, (2, IMGS, 3, 72, CH), (2, IMGS, 72, CH), (2, IMGS, 64, CH))
         ] + [pltpu.VMEM(shape, BF16) for shape in ((4, IMGS, ROWS, 16, CH), cols, cols, cols, cols, (4, IMGS, 3, 16, CH))
-        ] + [pltpu.VMEM(shape, F32) for shape in ((18 * CH, CH), (18 * CH, CH), *((size, CH) for _, size in CHAINS))
-        ] + [pltpu.SemaphoreType.DMA(shape) for shape in ((IMGS, 3), (CHUNKS,), (4,), (10,), (10,), (3 * CHAIN_SEMS,), (3 * CHAIN_SEMS,))],
-        compiler_params=pltpu.CompilerParams(collective_id=0, has_side_effects=True, vmem_limit_bytes=67043328),
+        ] + [pltpu.VMEM(shape, F32) for shape in ((18 * CH, CH), *((size, CH) for _, size in CHAINS))
+        ] + [pltpu.SemaphoreType.DMA(shape) for shape in ((IMGS, 3), (4,), (10,), (10,), (3 * CHAIN_SEMS,), (3 * CHAIN_SEMS,))],
+        compiler_params=pltpu.CompilerParams(collective_id=0, has_side_effects=True, vmem_limit_bytes=BLOCK_BYTES),
         name="block_grads",
     )(x_tile, a_tile, g_tile, w_one, w_two)
 

time: 77.5 us -> 70.9 us (0.915)
  Pallas kernels: 76.8 us -> 70.1 us
    pallas_call x1, Pallas kernels: 72 us -> 67.5 us  [block_grads(): pl.pallas_call(functools.partial(block_kernel, mesh_shape['row'], mesh_sh...]
    pallas_call x1, Pallas kernels: 4.73 us -> 2.58 us  [place_results(): pl.pallas_call(place_kernel, out_shape=[jax.ShapeDtypeStruct((IMGS, ROWS,...]
where the time goes in v3:
time: 70.9 us; the launch traced here: 70.8 us
  Pallas kernels  70.1 us (99%)
    pallas_call x1, Pallas kernels, block_grads(): pl.pallas_call(functools.partial(block_kernel, mesh_shape['row'], mesh_sh...  67.5 us
    pallas_call x1, Pallas kernels, place_results(): pl.pallas_call(place_kernel, out_shape=[jax.ShapeDtypeStruct((IMGS, ROWS,...  2.58 us

profile of v3, /device:TPU:0, one launch (start us, length us, event | category | flops | bytes accessed | tf_op | source)
XLA Modules:
  0.0 70.8 jit_solution(17594698066407907314)
XLA Ops:
  0.6 67.5 %block_grads.1 = (bf16[2,48,192,128]{3,2,1,0:T(8,128)(2,1)S(1)}, f32[2304,128]{1,0:T(8,128)S(1)}) custom-call(bf16[2,48,192,128]{3,2,1,0:T(8,128)(2,1)} %x_hbm.1, bf16[2,48,192,128]{3,2,1,0:T(8,128)(2,1)} %a_hbm.1, bf16[2,48,192,128]{3,2,1,0:T(8,128)(2,1)} %g_hbm.1, bf16[3,3,128,128]{3,2,1,0:T(8,128)(2,1)} %w1.1, bf16[3,3,128,128]{3,2,1,0:T(8,128)(2,1)} %w2.1), custom_call_target="tpu_custom_call" | custom-call | tf_op jit(solution)/shard_map/block_grads/pallas_call | solution.py:460
  68.2 2.6 %place_results.1 = (bf16[2,48,192,128]{3,2,1,0:T(8,128)(2,1)}, f32[1152,128]{1,0:T(8,128)}, f32[1152,128]{1,0:T(8,128)}) custom-call(bf16[2,48,192,128]{3,2,1,0:T(8,128)(2,1)S(1)} %get-tuple-element.8.dx_in, f32[2304,128]{1,0:T(8,128)S(1)} %get-tuple-element.9.dw_in), custom_call_target="tpu_custom_call" | custom-call | tf_op jit(solution)/shard_map/place_results/pallas_call | solution.py:444

commit v4 on v3

--- a/solution.py
+++ b/solution.py
@@ -415,16 +415,16 @@
     conv_x(0, dz0)
 
     def step_c(i, carry):
-        at_steps(i, ((1, chain0, 3), (3, chain0, 4), (4, chain1, 4), (5, chain0, 5)))
+        at_steps(i, ((1, chain0, 3), (2, chain2, 2), (3, chain0, 4), (4, chain2, 3), (5, chain0, 5)))
         conv_x(2 * i + 1, dz1)
         finish(2 * i, dz0)
-        at_steps(i, ((0, chain2, 1), (0, chain1, 2), (2, chain2, 2), (2, chain1, 3), (4, chain2, 3)))
+        at_steps(i, ((0, chain2, 1), (0, chain1, 2), (2, chain1, 3), (4, chain1, 4), (5, chain2, 4)))
         conv_x(jnp.minimum(2 * i + 2, CHUNKS - 1), dz0)
         finish(2 * i + 1, dz1)
         return carry
 
     lax.fori_loop(0, CHUNKS // 2, step_c, 0)
-    for chain, k in ((chain1, 5), (chain2, 4), (chain0, 6), (chain1, 6), (chain2, 5), (chain2, 6)):
+    for chain, k in ((chain1, 5), (chain0, 6), (chain2, 5), (chain1, 6), (chain2, 6)):
         chain(k)
 
 

time: 70.9 us -> 69.3 us (0.977)
  Pallas kernels: 70.1 us -> 68.5 us
    pallas_call x1, Pallas kernels: 67.5 us -> 65.9 us  [block_grads(): pl.pallas_call(functools.partial(block_kernel, mesh_shape['row'], mesh_sh...]
where the time goes in v4:
time: 69.3 us; the launch traced here: 69.2 us
  Pallas kernels  68.5 us (99%)
    pallas_call x1, Pallas kernels, block_grads(): pl.pallas_call(functools.partial(block_kernel, mesh_shape['row'], mesh_sh...  65.9 us
    pallas_call x1, Pallas kernels, place_results(): pl.pallas_call(place_kernel, out_shape=[jax.ShapeDtypeStruct((IMGS, ROWS,...  2.58 us

profile of v4, /device:TPU:0, one launch (start us, length us, event | category | flops | bytes accessed | tf_op | source)
XLA Modules:
  0.0 69.2 jit_solution(4611718477832238509)
XLA Ops:
  0.6 65.9 %block_grads.1 = (bf16[2,48,192,128]{3,2,1,0:T(8,128)(2,1)S(1)}, f32[2304,128]{1,0:T(8,128)S(1)}) custom-call(bf16[2,48,192,128]{3,2,1,0:T(8,128)(2,1)} %x_hbm.1, bf16[2,48,192,128]{3,2,1,0:T(8,128)(2,1)} %a_hbm.1, bf16[2,48,192,128]{3,2,1,0:T(8,128)(2,1)} %g_hbm.1, bf16[3,3,128,128]{3,2,1,0:T(8,128)(2,1)} %w1.1, bf16[3,3,128,128]{3,2,1,0:T(8,128)(2,1)} %w2.1), custom_call_target="tpu_custom_call" | custom-call | tf_op jit(solution)/shard_map/block_grads/pallas_call | solution.py:460
  66.6 2.6 %place_results.1 = (bf16[2,48,192,128]{3,2,1,0:T(8,128)(2,1)}, f32[1152,128]{1,0:T(8,128)}, f32[1152,128]{1,0:T(8,128)}) custom-call(bf16[2,48,192,128]{3,2,1,0:T(8,128)(2,1)S(1)} %get-tuple-element.8.dx_in, f32[2304,128]{1,0:T(8,128)S(1)} %get-tuple-element.9.dw_in), custom_call_target="tpu_custom_call" | custom-call | tf_op jit(solution)/shard_map/place_results/pallas_call | solution.py:444
